TPU v7x, 32 devices: a whole 2x2x4 slice. The times are simulated.
32 devices in a mesh: dom: 8 (over z, x), feat: 4 (over y, core).
Axes of the slice: x: 2, y: 2, z: 4, core: 2. Of those that a mesh axis runs over, the one named last changes fastest.
Arguments:
- feats: bfloat16 [256, 4096], P('feat', 'dom'), may hold values from -6 to 6
- self_weight: bfloat16 [256, 256], P(None, 'feat'), may hold values from -0.375 to 0.375
- bases: bfloat16 [30, 256, 256], P(None, 'feat'), may hold values from -0.375 to 0.375
- coef: float32 [237, 30], replicated, may hold values from -1.2 to 1.2
- src_part: int32 [8192, 1], P('dom'), may hold values from 0 to 7; in each aligned block of 1024 rows (0 to 1023, 1024 to 2047, ...) at most 256 rows name the same one
- src_row: int32 [8192], P('dom'), may hold values from 0 to 511
- edge_dst: int32 [8192], P('dom'), may hold values from 0 to 511
- edge_rel: int32 [8192], P('dom'), may hold values from 0 to 236
- block_owner: int32 [64, 1], P('dom'), may hold values from 0 to 7; in each aligned block of 8 rows (0 to 7, 8 to 15, ...) at most 2 rows name the same one
- block_valid: int32 [8, 8], P('dom'), may hold values from 1 to 128, 896 in all within a row
- cotangent: bfloat16 [256, 4096], P('feat', 'dom'), may hold values from -6 to 6
Outputs:
- output: bfloat16 [256, 4096], P('feat', 'dom')
- grad_feats: bfloat16 [256, 4096], P('feat', 'dom')
- grad_bases: float32 [30, 256, 256], P(None, 'feat')
- grad_self: float32 [256, 256], P(None, 'feat')
- grad_coef: float32 [237, 30], replicated
Inputs may be any that keep to these rules, and one draw needn't show every extreme that they name: `src_part`: among the edge rows of one index of dom, no partition is the source partition of more than 256 rows, and some partition of exactly 256. `block_owner`: among the blocks of one index of dom, no partition owns more than 2, a bound that some block reaches. `block_valid`: the valid rows of a block come first; the counts of one index of dom sum to 896.
All inputs are finite; a program needn't handle non-finite values.
Results may differ from a plain program's by a relative error of at most 0.0055.
Values may be sent and summed in bfloat16 or wider, within the bound.
A program may use at most 64 MiB of HBM per device.

v0:
```python
import jax
import jax.numpy as jnp
from jax import lax
from jax.sharding import PartitionSpec as P


def body(
    feats,
    self_weight,
    bases,
    coef,
    src_part,
    src_row,
    edge_dst,
    edge_rel,
    block_owner,
    block_valid,
    cotangent,
):
    dom_count = lax.axis_size("dom")
    quarter = feats.shape[0]
    entities = feats.shape[1]
    edge_count = src_row.shape[0]
    block_count = block_valid.shape[1]
    block_rows = edge_count // block_count
    slot_cap = 128 * ((2 * edge_count + 128 * dom_count - 1) // (128 * dom_count))
    block_cap = (2 * block_count + dom_count - 1) // dom_count
    basis_count = bases.shape[0]
    model_width = bases.shape[2]
    relation_count = coef.shape[0]
    block_span = min(512, edge_count)
    block_total = edge_count // block_span
    live_rows = (jnp.arange(block_rows)[None, :] < block_valid[0][:, None]).reshape(edge_count)
    source_part = src_part[:, 0]
    onehot_float = (source_part[:, None] == jnp.arange(dom_count)[None, :]).astype(jnp.float32)
    onehot_float = onehot_float.reshape(block_count, block_rows, dom_count)
    before = (jnp.arange(block_rows)[None, :] < jnp.arange(block_rows)[:, None]).astype(jnp.float32)
    inside = jnp.einsum("jk,bkp->bjp", before, onehot_float, precision=lax.Precision.HIGHEST)
    totals = jnp.sum(onehot_float, axis=1)
    offsets = jnp.cumsum(totals, axis=0) - totals
    slot_rank = (
        jnp.sum((inside + offsets[:, None, :]) * onehot_float, axis=2)
        .reshape(edge_count)
        .astype(jnp.int32)
    )
    slot_index = source_part * slot_cap + slot_rank
    requests = jnp.full((dom_count * slot_cap,), entities, jnp.int32).at[slot_index].set(src_row)
    requests = requests.reshape(dom_count, slot_cap)
    owners = block_owner[:, 0]
    owner_hot = (owners[:, None] == jnp.arange(dom_count)[None, :]).astype(jnp.int32)
    block_rank = jnp.sum((jnp.cumsum(owner_hot, axis=0) - owner_hot) * owner_hot, axis=1)
    block_slot = owners * block_cap + block_rank
    dst_rows = jnp.where(live_rows, edge_dst, entities).reshape(block_count, block_rows)
    dst_send = (
        jnp.full((dom_count * block_cap, block_rows), entities, jnp.int32)
        .at[block_slot]
        .set(dst_rows)
    )
    dst_send = dst_send.reshape(dom_count, block_cap * block_rows)
    asked_rows, arriving = (
        lax.all_to_all(requests, "dom", split_axis=0, concat_axis=0, tiled=True),
        lax.all_to_all(dst_send, "dom", split_axis=0, concat_axis=0, tiled=True),
    )
    served = jnp.take(feats, asked_rows, axis=1, mode="fill", fill_value=0)
    fetched = lax.all_to_all(served, "dom", split_axis=1, concat_axis=1, tiled=True).reshape(
        quarter, dom_count * slot_cap
    )
    source_quarter = jnp.take(fetched, slot_index, axis=1)
    sources, own_full = (
        lax.all_gather(source_quarter, "feat", axis=0, tiled=True),
        lax.all_gather(feats, "feat", axis=0, tiled=True),
    )
    bases_flat = bases.reshape(basis_count * quarter, model_width)

    def block_weights(offset):
        relation_block = lax.dynamic_slice_in_dim(edge_rel, offset, block_span, 0)
        relation_hot = (relation_block[:, None] == jnp.arange(relation_count)[None, :]).astype(
            jnp.float32
        )
        weights = jnp.dot(relation_hot, coef, precision=lax.Precision.HIGHEST)
        return (relation_hot, weights)

    def block_terms(offset):
        source_block = lax.dynamic_slice_in_dim(sources, offset, block_span, 1)
        products = lax.dot_general(
            source_block, bases_flat, (((0,), (1,)), ((), ())), preferred_element_type=jnp.float32
        )
        relation_hot, weights = block_weights(offset)
        return (
            source_block,
            products.reshape(block_span, basis_count, quarter),
            relation_hot,
            weights,
        )

    def forward_step(step_index, messages):
        offset = step_index * block_span
        source_block, products, relation_hot, weights = block_terms(offset)
        live_block = lax.dynamic_slice_in_dim(live_rows, offset, block_span, 0)
        mixed = jnp.einsum("eb,ebo->oe", weights, products, precision=lax.Precision.HIGHEST)
        mixed = jnp.where(live_block[None, :], mixed, 0.0).astype(jnp.bfloat16)
        return lax.dynamic_update_slice_in_dim(messages, mixed, offset, 1)

    messages = lax.fori_loop(
        0, block_total, forward_step, jnp.zeros((quarter, edge_count), jnp.bfloat16)
    )
    message_send = jnp.zeros((quarter, dom_count * block_cap, block_rows), jnp.bfloat16)
    message_send = message_send.at[:, block_slot].set(
        messages.reshape(quarter, block_count, block_rows)
    )
    message_send = message_send.reshape(quarter, dom_count, block_cap * block_rows)
    received = lax.all_to_all(message_send, "dom", split_axis=1, concat_axis=1, tiled=True)
    aggregate = (
        jnp.zeros((quarter, entities), jnp.float32)
        .at[:, arriving]
        .add(received.astype(jnp.float32), mode="drop")
    )
    degree = jnp.zeros((entities,), jnp.float32).at[arriving].add(1.0, mode="drop")
    inverse_degree = 1.0 / jnp.maximum(degree, 1.0)
    preact = lax.dot_general(
        self_weight, own_full, (((0,), (0,)), ((), ())), preferred_element_type=jnp.float32
    )
    preact = preact + inverse_degree[None, :] * aggregate
    output = jax.nn.silu(preact).astype(jnp.bfloat16)
    sigmoid_pre = jax.nn.sigmoid(preact)
    grad_pre = (
        cotangent.astype(jnp.float32) * sigmoid_pre * (1.0 + preact * (1.0 - sigmoid_pre))
    ).astype(jnp.bfloat16)
    sent_back = jnp.take(grad_pre, arriving, axis=1, mode="fill", fill_value=0).astype(jnp.float32)
    sent_back = (
        sent_back * jnp.take(inverse_degree, arriving, mode="fill", fill_value=0.0)[None]
    ).astype(jnp.bfloat16)
    returned = lax.all_to_all(sent_back, "dom", split_axis=1, concat_axis=1, tiled=True)
    grad_message = returned.reshape(quarter, dom_count * block_cap, block_rows)[
        :, block_slot
    ].reshape(quarter, edge_count)

    def backward_step(step_index, totals_now):
        grad_bases, grad_coef, edge_partial = totals_now
        offset = step_index * block_span
        source_block, products, relation_hot, weights = block_terms(offset)
        grad_block = lax.dynamic_slice_in_dim(grad_message, offset, block_span, 1).astype(
            jnp.float32
        )
        scaled = jnp.einsum("ebo,oe->eb", products, grad_block, precision=lax.Precision.HIGHEST)
        grad_coef = grad_coef + lax.dot_general(
            relation_hot, scaled, (((0,), (0,)), ((), ())), precision=lax.Precision.HIGHEST
        )
        combined = (weights[:, :, None] * grad_block.T[:, None, :]).astype(jnp.bfloat16)
        combined = combined.reshape(block_span, basis_count * quarter)
        grad_bases = grad_bases + lax.dot_general(
            combined, source_block, (((0,), (1,)), ((), ())), preferred_element_type=jnp.float32
        )
        partial_grad = lax.dot_general(
            bases_flat, combined, (((0,), (1,)), ((), ())), preferred_element_type=jnp.float32
        )
        edge_partial = lax.dynamic_update_slice_in_dim(edge_partial, partial_grad, offset, 1)
        return (grad_bases, grad_coef, edge_partial)

    start_state = (
        jnp.zeros((basis_count * quarter, model_width), jnp.float32),
        jnp.zeros((relation_count, basis_count), jnp.float32),
        jnp.zeros((model_width, edge_count), jnp.float32),
    )
    grad_bases, grad_coef, edge_partial = lax.fori_loop(0, block_total, backward_step, start_state)
    self_partial = jnp.dot(self_weight, grad_pre, preferred_element_type=jnp.float32)
    edge_grads, self_grads = (
        lax.psum_scatter(edge_partial, "feat", scatter_dimension=0, tiled=True),
        lax.psum_scatter(self_partial, "feat", scatter_dimension=0, tiled=True),
    )
    slot_grads = (
        jnp.zeros((quarter, dom_count * slot_cap), jnp.float32).at[:, slot_index].set(edge_grads)
    )
    slot_grads = slot_grads.reshape(quarter, dom_count, slot_cap)
    arrived_grads = lax.all_to_all(slot_grads, "dom", split_axis=1, concat_axis=1, tiled=True)
    source_sum = (
        jnp.zeros((quarter, entities), jnp.float32)
        .at[:, asked_rows]
        .add(arrived_grads, mode="drop")
    )
    grad_feats = (self_grads + source_sum).astype(jnp.bfloat16)
    self_term = lax.dot_general(
        own_full, grad_pre, (((1,), (1,)), ((), ())), preferred_element_type=jnp.float32
    )
    scale = float(edge_count * dom_count) ** (-0.5)
    bases_total, self_total = lax.psum((grad_bases, self_term), "dom")
    coef_total = lax.psum(grad_coef, ("dom", "feat"))
    return (
        output,
        grad_feats,
        (bases_total * scale).reshape(basis_count, quarter, model_width),
        self_total * scale,
        coef_total * scale,
    )


def solution(mesh):
    return jax.shard_map(
        body,
        mesh=mesh,
        in_specs=(
            P("feat", "dom"),
            P(None, "feat"),
            P(None, "feat", None),
            P(),
            P("dom", None),
            P("dom"),
            P("dom"),
            P("dom"),
            P("dom", None),
            P("dom", None),
            P("feat", "dom"),
        ),
        out_specs=(P("feat", "dom"), P("feat", "dom"), P(None, "feat", None), P(None, "feat"), P()),
        check_vma=False,
    )
```

profile of v0, /device:TPU:0, one launch (start us, length us, event | category | flops | bytes accessed | tf_op | source)
XLA Modules:
  0.0 305.0 jit_solution(917960564627141620)
XLA Ops:
  10.5 5.0 %scatter_custom_fusion.2 = s32[2048]{0:T(1024)} fusion(s32[1024]{0:T(1024)S(1)} %bitcast.176, s32[1024]{0:T(1024)} %param.22, s32[]{:T(128)} %constant.135.clone.1), kind=kCustom, calls=%fused_computation.85 | custom fusion | bytes 8704 | tf_op jit(solution)/shard_map/scatter | solution.py:47
  15.5 7.3 %all-to-all-start.1 = ((s32[8,1,256]{2,1,0:T(1,128)}), s32[8,1,256]{2,1,0:T(1,128)S(1)}, u32[]{:S(2)}, u32[]{:S(2)}) async-start(s32[8,1,256]{2,1,0:T(1,128)} %bitcast.18), calls=%async_computation.1 | async-start | bytes 16384 | tf_op jit(solution)/shard_map/all_to_all | solution.py:61
  25.8 6.0 %all_gather.6 = bf16[256,512]{1,0:T(8,128)(2,1)S(1)} all-gather(bf16[64,512]{1,0:T(8,128)(2,1)} %param.17), channel_id=1, replica_groups=mesh['dom'=8,'feat'=4] {'feat'}, dimensions={0}, use_global_device_ids=true | all-gather | bytes 327680 | tf_op jit(solution)/shard_map/all_gather | solution.py:71
  31.8 1.0 copy.90
  32.8 1.4 scatter_custom_fusion
  34.2 6.0 %all-to-all-start = ((s32[8,1,256]{2,1,0:T(1,128)}), s32[8,1,256]{2,1,0:T(1,128)S(1)}, u32[]{:S(2)}, u32[]{:S(2)}) async-start(s32[8,1,256]{2,1,0:T(1,128)} %bitcast.10), calls=%async_computation | async-start | bytes 16384 | tf_op jit(solution)/shard_map/all_to_all | solution.py:62
  40.2 6.2 %gather_fusion.3 = bf16[2048,64]{1,0:T(8,128)(2,1)S(1)} fusion(bf16[64,512]{0,1:T(8,128)(2,1)S(1)} %copy.90, s32[2048]{0:T(1024)S(1)} %broadcast_clamp_fusion.2), kind=kCustom, calls=%fused_computation.clone | custom fusion | bytes 532480 | tf_op jit(solution)/shard_map/jit(_take)/gather | solution.py:64
  47.4 6.0 %all-to-all-start.2 = ((bf16[64,8,256]{2,0,1:T(8,128)(2,1)}), bf16[64,8,256]{2,0,1:T(8,128)(2,1)S(1)}, u32[]{:S(2)}, u32[]{:S(2)}) async-start(bf16[64,8,256]{2,0,1:T(8,128)(2,1)} %select_bitcast_fusion), calls=%async_computation.2 | async-start | bytes 524288 | tf_op jit(solution)/shard_map/all_to_all | solution.py:65
  53.4 14.7 %scatter_custom_fusion.1 = f32[512]{0:T(512)S(1)} fusion(s32[2048]{0:T(1024)S(1)} %bitcast.169, f32[2048]{0:T(1024)S(1)} %broadcast.150, f32[]{:T(128)} %constant.134.clone.1), kind=kCustom, calls=%fused_computation.98 | custom fusion | flops 2048 | bytes 2052 | tf_op jit(solution)/shard_map/scatter-add | solution.py:118
  68.4 3.2 %gather_fusion = bf16[1024,64]{1,0:T(8,128)(2,1)S(1)} fusion(bf16[64,2048]{0,1:T(8,128)(2,1)S(1)} %bitcast.160, s32[1024]{0:T(1024)S(1)} %broadcast_clamp_fusion.3), kind=kCustom, calls=%fused_computation.2 | custom fusion | bytes 266240 | tf_op jit(solution)/shard_map/jit(_take)/gather | solution.py:68
  72.0 7.2 %all_gather.7 = bf16[256,1024]{1,0:T(8,128)(2,1)S(1)} all-gather(bf16[64,1024]{1,0:T(8,128)(2,1)S(1)} %copy.93), channel_id=1, replica_groups=mesh['dom'=8,'feat'=4] {'feat'}, dimensions={0}, use_global_device_ids=true | all-gather | bytes 655360 | tf_op jit(solution)/shard_map/all_gather | solution.py:70
  79.2 3.9 %while.31 = (s32[]{:T(128)}, bf16[64,1024]{1,0:T(8,128)(2,1)S(1)}, pred[1024]{0:T(1024)(128)(4,1)S(1)}, bf16[256,1024]{1,0:T(8,128)(2,1)S(1)}, bf16[1920,256]{1,...) while((s32[]{:T(128)}, bf16[64,1024]{1,0:T(8,128)(2,1)S(1)}, ...), condition=%wide.region_9.11_spmd, body=%wide.region_8.10_spmd.sunk | while | flops 549087744 | bytes 9465283 | solution.py:104
  85.0 6.0 %all-to-all-start.3 = ((bf16[64,8,256]{2,0,1:T(8,128)(2,1)}), bf16[64,8,256]{2,0,1:T(8,128)(2,1)S(1)}, u32[]{:S(2)}, u32[]{:S(2)}) async-start(bf16[64,8,256]{2,0,1:T(8,128)(2,1)} %copy.96), calls=%async_computation.3 | async-start | bytes 524288 | tf_op jit(solution)/shard_map/all_to_all | solution.py:112
  91.0 13.2 %gather_fusion.1 = f32[2048]{0:T(1024)S(1)} fusion(f32[512]{0:T(512)S(1)} %maximum_divide_fusion, s32[2048]{0:T(1024)S(1)} %broadcast_clamp_fusion), kind=kCustom, calls=%fused_computation.3 | custom fusion | bytes 24576 | tf_op jit(solution)/shard_map/jit(_take)/gather | solution.py:131
  104.6 11.5 %scatter_custom_fusion.4 = f32[64,512]{0,1:T(8,128)S(1)} fusion(s32[2048]{0:T(1024)S(1)} %bitcast.171, f32[2048,64]{1,0:T(8,128)S(1)} %bitcast.167, f32[]{:T(128)} %constant.134.clone.1), kind=kCustom, calls=%fused_computation.59 | custom fusion | flops 131072 | bytes 131076 | tf_op jit(solution)/shard_map/scatter-add | solution.py:116
  117.9 6.2 %gather_fusion.4 = bf16[2048,64]{1,0:T(8,128)(2,1)S(1)} fusion(bf16[64,512]{0,1:T(8,128)(2,1)S(1)} %copy.100, s32[2048]{0:T(1024)S(1)} %broadcast_clamp_fusion.1), kind=kCustom, calls=%fused_computation.1.clone | custom fusion | bytes 532480 | tf_op jit(solution)/shard_map/jit(_take)/gather | solution.py:129
  125.1 6.0 %all-to-all-start.4 = ((bf16[64,8,256]{2,0,1:T(8,128)(2,1)}), bf16[64,8,256]{2,0,1:T(8,128)(2,1)}, u32[]{:S(2)}, u32[]{:S(2)}) async-start(bf16[64,8,256]{2,0,1:T(8,128)(2,1)} %multiply_convert_fusion.1), calls=%async_computation.4 | async-start | bytes 524288 | tf_op jit(solution)/shard_map/all_to_all | solution.py:133
  132.0 8.1 %all-to-all-done.4 = bf16[64,8,256]{2,0,1:T(8,128)(2,1)} async-done(((bf16[64,8,256]{2,0,1:T(8,128)(2,1)}), bf16[64,8,256]{2,0,1:T(8,128)(2,1)}, u32[]{:S(2)}, u32[]{:S(2)}) %all-to-all-start.4) | async-done | bytes 262176 | tf_op jit(solution)/shard_map/all_to_all | solution.py:133
  140.1 1.8 copy.102
  141.9 1.7 reshape.216
  143.6 1.7 copy.103
  145.3 2.1 gather_fusion.2
  147.5 1.6 copy_bitcast_fusion
  149.0 1.1 broadcast_in_dim.132.clone
  150.1 21.8 %while.32 = (s32[]{:T(128)}, f32[1920,256]{1,0:T(8,128)S(1)}, f32[237,30]{0,1:T(8,128)S(1)}, f32[256,1024]{1,0:T(8,128)}, s32[1024]{0:T(1024)S(1)}, /*index=5*/f...) while((s32[]{:T(128)}, f32[1920,256]{1,0:T(8,128)S(1)}, ...), condition=%wide.region_14.16_spmd.clone, body=%wide.region_13.15_spmd.clone.sunk | while | flops 1602539392 | bytes 28454508 | solution.py:165
  150.2 1.2 fusion.87
  151.4 1.5 bitcast_convert_fusion.2
  153.5 1.5 convolution_bitcast_fusion.4
  155.0 1.2 convolution_add_fusion.6
  156.2 1.2 copy.156
  158.3 1.6 fusion.88
  161.1 1.2 fusion.87
  162.3 1.5 bitcast_convert_fusion.2
  164.4 1.5 convolution_bitcast_fusion.4
  165.9 1.2 convolution_add_fusion.6
  167.1 1.2 copy.156
  169.2 1.7 fusion.88
  172.0 1.4 convolution_bitcast_fusion.1
  175.4 41.2 %psum.23 = f32[237,30]{0,1:T(8,128)S(1)} all-reduce(f32[237,30]{0,1:T(8,128)S(1)} %get-tuple-element.289), channel_id=1, replica_groups=mesh['dom'=8,'feat'=4] {'dom','feat'}, use_global_device_ids=true, to_apply=%region_20.22 | all-reduce | flops 7110 | bytes 56880 | tf_op jit(solution)/shard_map/psum | solution.py:187
  216.6 1.1 copy.126
  217.8 3.5 %scatter_custom_fusion.5 = f32[64,2048]{0,1:T(8,128)S(1)} fusion(s32[1024]{0:T(1024)} %bitcast.178, f32[64,1024]{0,1:T(8,128)S(1)} %copy.126, f32[]{:T(128)} %constant.134.clone.1), kind=kCustom, calls=%fused_computation.47 | custom fusion | bytes 786944 | tf_op jit(solution)/shard_map/scatter | solution.py:172
  221.3 1.1 copy.105
  222.4 4.8 %all-to-all-start.5 = ((f32[64,8,256]{2,0,1:T(8,128)}), f32[64,8,256]{2,0,1:T(8,128)S(1)}, u32[]{:S(2)}, u32[]{:S(2)}) async-start(f32[64,8,256]{2,0,1:T(8,128)} %copy.105), calls=%async_computation.5 | async-start | bytes 1048576 | tf_op jit(solution)/shard_map/all_to_all | solution.py:175
  227.9 1.0 copy.124
  228.9 51.5 %all-reduce.3.cloned.1.call-done = (f32[1920,256]{1,0:T(8,128)}, f32[256,64]{0,1:T(8,128)}) async-done(((f32[1920,256]{1,0:T(8,128)}, f32[256,64]{0,1:T(8,128)}), (f32[1920,256]{1,0:T(8,128)}, f32[256,64]{0,1:T(8,128)})) %all-reduce.3.cloned.1.call-update) | async-done | bytes 2031632 | tf_op jit(solution)/shard_map/psum | solution.py:186
  280.4 1.5 broadcast_multiply_fusion.1
  281.9 3.0 broadcast_multiply_fusion
  285.2 11.6 %scatter_fusion.1 = f32[64,512]{0,1:T(8,128)S(1)} fusion(f32[64,512]{0,1:T(8,128)S(1)} %copy.124, s32[2048]{0:T(1024)S(1)} %bitcast.168, f32[2048,64]{1,0:T(8,128)S(1)} %bitcast.162), kind=kCustom, calls=%fused_computation.11 | custom fusion | flops 131072 | bytes 1581056 | tf_op jit(solution)/shard_map/scatter-add | solution.py:179
  (125 shorter events, 25.4 us)
Async XLA Ops:
  8.0 108.3 %copy-start = (bf16[256,64]{0,1:T(8,128)(2,1)S(1)}, bf16[256,64]{0,1:T(8,128)(2,1)}, u32[]{:S(2)}) copy-start(bf16[256,64]{0,1:T(8,128)(2,1)} %param.18) | copy-start | bytes 98308
  10.5 13.1 %copy-start.11 = (s32[1024,1]{0,1:T(1,128)}, s32[1024,1]{0,1:T(1,128)S(1)}, u32[]{:S(2)}) copy-start(s32[1024,1]{0,1:T(1,128)S(1)} %get-tuple-element.435) | copy-start | bytes 12292
  15.5 18.6 %all-to-all-start.1 = ((s32[8,1,256]{2,1,0:T(1,128)}), s32[8,1,256]{2,1,0:T(1,128)S(1)}, u32[]{:S(2)}, u32[]{:S(2)}) async-start(s32[8,1,256]{2,1,0:T(1,128)} %bitcast.18), calls=%async_computation.1 | async-start | bytes 16384 | tf_op jit(solution)/shard_map/all_to_all | solution.py:61
  25.8 57.4 %copy-start.12 = (s32[8]{0:T(128)}, s32[8]{0:T(128)S(1)}, u32[]{:S(2)}) copy-start(s32[8]{0:T(128)S(1)} %fusion.39) | copy-start | bytes 100
  31.8 84.5 %copy-start.6 = (bf16[256,512]{1,0:T(8,128)(2,1)}, bf16[256,512]{1,0:T(8,128)(2,1)S(1)}, u32[]{:S(2)}) copy-start(bf16[256,512]{1,0:T(8,128)(2,1)S(1)} %all_gather.6) | copy-start | bytes 786436
  34.2 13.2 %all-to-all-start = ((s32[8,1,256]{2,1,0:T(1,128)}), s32[8,1,256]{2,1,0:T(1,128)S(1)}, u32[]{:S(2)}, u32[]{:S(2)}) async-start(s32[8,1,256]{2,1,0:T(1,128)} %bitcast.10), calls=%async_computation | async-start | bytes 16384 | tf_op jit(solution)/shard_map/all_to_all | solution.py:62
  47.4 20.7 %all-to-all-start.2 = ((bf16[64,8,256]{2,0,1:T(8,128)(2,1)}), bf16[64,8,256]{2,0,1:T(8,128)(2,1)S(1)}, u32[]{:S(2)}, u32[]{:S(2)}) async-start(bf16[64,8,256]{2,0,1:T(8,128)(2,1)} %select_bitcast_fusion), calls=%async_computation.2 | async-start | bytes 524288 | tf_op jit(solution)/shard_map/all_to_all | solution.py:65
  53.3 25.8 %copy-start.1 = (bf16[30,64,256]{2,1,0:T(8,128)(2,1)S(1)}, bf16[30,64,256]{2,1,0:T(8,128)(2,1)}, u32[]{:S(2)}) copy-start(bf16[30,64,256]{2,1,0:T(8,128)(2,1)} %param.19) | copy-start | bytes 2949124
  53.4 25.8 %copy-start.10 = (s32[1024]{0:T(1024)S(1)}, s32[1024]{0:T(1024)}, u32[]{:S(2)}) copy-start(s32[1024]{0:T(1024)} %param.24) | copy-start | bytes 12292
  53.4 25.8 %copy-start.14 = (f32[237,30]{0,1:T(8,128)S(1)}, f32[237,30]{0,1:T(8,128)}, u32[]{:S(2)}) copy-start(f32[237,30]{0,1:T(8,128)} %param.20) | copy-start | bytes 85324
  85.0 19.3 %all-to-all-start.3 = ((bf16[64,8,256]{2,0,1:T(8,128)(2,1)}), bf16[64,8,256]{2,0,1:T(8,128)(2,1)S(1)}, u32[]{:S(2)}, u32[]{:S(2)}) async-start(bf16[64,8,256]{2,0,1:T(8,128)(2,1)} %copy.96), calls=%async_computation.3 | async-start | bytes 524288 | tf_op jit(solution)/shard_map/all_to_all | solution.py:112
  104.2 12.1 %copy-start.13 = (bf16[64,512]{1,0:T(8,128)(2,1)S(1)}, bf16[64,512]{1,0:T(8,128)(2,1)}, u32[]{:S(2)}) copy-start(bf16[64,512]{1,0:T(8,128)(2,1)} %param.27) | copy-start | bytes 196612
  117.2 0.6 copy-start.8
  125.1 15.0 %all-to-all-start.4 = ((bf16[64,8,256]{2,0,1:T(8,128)(2,1)}), bf16[64,8,256]{2,0,1:T(8,128)(2,1)}, u32[]{:S(2)}, u32[]{:S(2)}) async-start(bf16[64,8,256]{2,0,1:T(8,128)(2,1)} %multiply_convert_fusion.1), calls=%async_computation.4 | async-start | bytes 524288 | tf_op jit(solution)/shard_map/all_to_all | solution.py:133
  131.1 85.6 %reduce-scatter.9.cloned.1.call-start = ((), (), s32[]{:S(2)}) async-start(), calls=%async_computation.9 | async-start | bytes 1310720
  150.1 4.9 %copy-start.3 = (bf16[256,1024]{1,0:T(8,128)(2,1)}, bf16[256,1024]{1,0:T(8,128)(2,1)S(1)}, u32[]{:S(2)}) copy-start(bf16[256,1024]{1,0:T(8,128)(2,1)S(1)} %get-tuple-element.608) | copy-start | bytes 1572868 | tf_op jit(solution)/shard_map/while
  158.3 1.7 copy-start.5
  160.0 1.0 copy-start.4
  161.0 4.9 %copy-start.3 = (bf16[256,1024]{1,0:T(8,128)(2,1)}, bf16[256,1024]{1,0:T(8,128)(2,1)S(1)}, u32[]{:S(2)}) copy-start(bf16[256,1024]{1,0:T(8,128)(2,1)S(1)} %get-tuple-element.608) | copy-start | bytes 1572868 | tf_op jit(solution)/shard_map/while
  169.2 1.7 copy-start.5
  170.9 1.0 copy-start.4
  171.9 3.4 %copy-start.2 = (f32[1920,256]{1,0:T(8,128)}, f32[1920,256]{1,0:T(8,128)S(1)}, u32[]{:S(2)}) copy-start(f32[1920,256]{1,0:T(8,128)S(1)} %get-tuple-element.288) | copy-start | bytes 5898244
  171.9 2.6 copy-start.7
  171.9 2.6 copy-start.9
  171.9 55.9 %reduce-scatter.7.cloned.1.call-start = ((), (), s32[]{:S(2)}) async-start(), calls=%async_computation.8 | async-start | bytes 655360
  174.4 106.0 %all-reduce.3.cloned.1.call-start = ((), (), s32[]{:S(2)}) async-start(), calls=%async_computation.10 | async-start | bytes 4063232 | tf_op jit(solution)/shard_map/psum | solution.py:186
  222.4 62.4 %all-to-all-start.5 = ((f32[64,8,256]{2,0,1:T(8,128)}), f32[64,8,256]{2,0,1:T(8,128)S(1)}, u32[]{:S(2)}, u32[]{:S(2)}) async-start(f32[64,8,256]{2,0,1:T(8,128)} %copy.105), calls=%async_computation.5 | async-start | bytes 1048576 | tf_op jit(solution)/shard_map/all_to_all | solution.py:175
Sparse Core Ops, SparseCore 0:
  172.1 23.2 reduce-scatter.8
  197.8 21.6 reduce-scatter.6
Sparse Core Ops, SparseCore 1:
  179.1 101.2 all-reduce.2
where the time goes:
time: 307 us; the launch traced here: 305 us
  local copies, waits for them, and re-layouts  62.4 us (20%)
  waiting for transfers between devices  59.7 us (19%)
  other arithmetic  57.8 us (19%)
  blocking collectives  54.4 us (18%)
  starting transfers between devices  36.3 us (12%)
  matrix products  18.1 us (6%)
  between operations  16 us (5%)
    psum x1, waiting for transfers between devices, body(): bases_total, self_total = lax.psum((grad_bases, self_term), 'dom')  51.5 us
    psum x1, blocking collectives, body(): coef_total = lax.psum(grad_coef, ('dom', 'feat'))  41.2 us
    scatter-add x1, other arithmetic, body(): jnp.zeros((entities,), jnp.float32).at[arriving].add(1.0, mode='drop')  14.7 us
    gather x2, local copies, waits for them, and re-layouts, body(): jnp.take(inverse_degree, arriving, mode='fill', fill_value=0.0)[None]  13.2 us
    scatter-add x1, other arithmetic, body(): source_sum = jnp.zeros((quarter, entities), jnp.float32).at[:, asked_rows...  11.6 us
    scatter-add x1, other arithmetic, body(): aggregate = jnp.zeros((quarter, entities), jnp.float32).at[:, arriving].a...  11.5 us
    all_to_all x1, waiting for transfers between devices, body(): lax.all_to_all(sent_back, 'dom', split_axis=1, concat_axis=1, tiled=True)  8.07 us
    all_to_all x1, starting transfers between devices, body(): lax.all_to_all(requests, 'dom', split_axis=0, concat_axis=0, tiled=True)  7.28 us
  transfers between devices with their start and end apart: 9, of which 2 were waited for; matrix products, arithmetic and copies ran while one was open for 18% of the time, Pallas kernels for 0%

commit v1 on v0

v1 whole, which is shorter than its diff:
```python
import jax
import jax.numpy as jnp
from jax import lax
from jax.sharding import PartitionSpec as P

BF = jnp.bfloat16
F32 = jnp.float32


def dot(left, right, left_axis, right_axis):
    return lax.dot_general(
        left, right, (((left_axis,), (right_axis,)), ((), ())), preferred_element_type=F32
    )


def onehot(ids, start, size):
    return (jnp.arange(size, dtype=jnp.int32)[:, None] + start == ids[None, :]).astype(BF)


def pick(table, ids, chunk):
    width = table.shape[1]
    if width <= chunk:
        return dot(table, onehot(ids, 0, width), 1, 0).astype(BF)

    def step(index, total):
        piece = lax.dynamic_slice_in_dim(table, index * chunk, chunk, 1)
        return total + dot(piece, onehot(ids, index * chunk, chunk), 1, 0)

    total = lax.fori_loop(
        0, width // chunk, step, jnp.zeros((table.shape[0], ids.shape[0]), F32)
    )
    return total.astype(BF)


def spread(values, ids, width, chunk):
    if width <= chunk:
        return dot(values, onehot(ids, 0, width), 1, 1)

    def step(index, total):
        piece = dot(values, onehot(ids, index * chunk, chunk), 1, 1)
        return lax.dynamic_update_slice_in_dim(total, piece, index * chunk, 1)

    return lax.fori_loop(0, width // chunk, step, jnp.zeros((values.shape[0], width), F32))


def scatter_sum(values, axis, count):
    rows = values.shape[0]
    parts = lax.all_to_all(values, axis, split_axis=1, concat_axis=0, tiled=True)
    return jnp.sum(parts.reshape(count, rows, -1).astype(F32), axis=0)


def body(
    feats,
    self_weight,
    bases,
    coef,
    src_part,
    src_row,
    edge_dst,
    edge_rel,
    block_owner,
    block_valid,
    cotangent,
):
    dom_count = lax.axis_size("dom")
    feat_count = lax.axis_size("feat")
    quarter, entities = feats.shape
    edge_count = src_row.shape[0]
    block_count = block_valid.shape[1]
    block_rows = edge_count // block_count
    basis_count, _, width = bases.shape
    relations = coef.shape[0]
    total_entities = dom_count * entities
    chunk = min(8, dom_count) * entities
    scale = float(edge_count * dom_count) ** (-0.5)

    source_ids = src_part[:, 0] * entities + src_row
    live = (jnp.arange(block_rows)[None, :] < block_valid[0][:, None]).reshape(edge_count)
    owners = jnp.broadcast_to(block_owner, (block_count, block_rows)).reshape(edge_count)
    target_ids = jnp.where(live, owners * entities + edge_dst, -1)
    relation_hot = onehot(edge_rel, 0, relations)

    table = lax.all_gather(feats, "dom", axis=1, tiled=True)
    source_quarter = pick(table, source_ids, chunk)
    gathered = lax.all_gather(
        jnp.concatenate([source_quarter, feats], axis=1), "feat", axis=0, tiled=True
    )
    sources = gathered[:, :edge_count]
    own_full = gathered[:, edge_count:]

    bases_flat = bases.reshape(basis_count * quarter, width)
    first = coef.astype(BF)
    second = (coef - first.astype(F32)).astype(BF)
    third = (coef - first.astype(F32) - second.astype(F32)).astype(BF)
    weights = (
        dot(first, relation_hot, 0, 0)
        + dot(second, relation_hot, 0, 0)
        + dot(third, relation_hot, 0, 0)
    )
    products = dot(bases_flat, sources, 1, 0).reshape(basis_count, quarter, edge_count)
    messages = jnp.sum(weights[:, None, :] * products, axis=0).astype(BF)
    extra = 16
    tail = jnp.zeros((extra, edge_count), BF).at[0].set(1.0)
    partial = spread(jnp.concatenate([messages, tail], axis=0), target_ids, total_entities, chunk)
    counted = partial[quarter:quarter + 1]
    high = jnp.floor(counted / 128.0)
    counts = jnp.concatenate(
        [high, counted - 128.0 * high, jnp.zeros((extra - 2, total_entities), F32)], axis=0
    )
    arrived = scatter_sum(
        jnp.concatenate([partial[:quarter], counts], axis=0).astype(BF), "dom", dom_count
    )
    aggregate = arrived[:quarter]
    degree = arrived[quarter:quarter + 1] * 128.0 + arrived[quarter + 1:quarter + 2]
    inverse_degree = 1.0 / jnp.maximum(degree, 1.0)
    preact = dot(self_weight, own_full, 0, 0) + inverse_degree * aggregate
    output = jax.nn.silu(preact).astype(BF)
    sigmoid_pre = jax.nn.sigmoid(preact)
    grad_pre = (
        cotangent.astype(F32) * sigmoid_pre * (1.0 + preact * (1.0 - sigmoid_pre))
    ).astype(BF)
    grad_node = (grad_pre.astype(F32) * inverse_degree).astype(BF)
    grad_table = lax.all_gather(grad_node, "dom", axis=1, tiled=True)
    grad_message = pick(grad_table, target_ids, chunk)

    grad_float = grad_message.astype(F32)
    scaled = jnp.sum(products * grad_float[None], axis=1)
    combined = (weights[:, None, :] * grad_float[None]).astype(BF)
    combined = combined.reshape(basis_count * quarter, edge_count)
    grad_bases = dot(combined, sources, 1, 1)
    edge_partial = dot(bases_flat, combined, 0, 0)
    self_partial = dot(self_weight, grad_pre, 1, 0)
    self_term = dot(grad_pre, own_full, 1, 1)
    both = jnp.concatenate([edge_partial, self_partial], axis=1).astype(BF)
    both = lax.all_to_all(both, "feat", split_axis=0, concat_axis=0, tiled=True)
    both = jnp.sum(both.reshape(feat_count, quarter, -1).astype(F32), axis=0)
    edge_grads = both[:, :edge_count].astype(BF)
    self_grads = both[:, edge_count:]
    node_grads = spread(edge_grads, source_ids, total_entities, chunk).astype(BF)
    grad_feats = (self_grads + scatter_sum(node_grads, "dom", dom_count)).astype(BF)

    stacked = jnp.concatenate([grad_bases, self_term], axis=0).astype(BF)
    pieces = lax.all_to_all(stacked, "dom", split_axis=0, concat_axis=0, tiled=True)
    piece = jnp.sum(pieces.reshape(dom_count, -1, width).astype(F32), axis=0) * scale
    whole = lax.all_gather(piece.astype(BF), "dom", axis=0, tiled=True).astype(F32)
    cut = basis_count * quarter

    scaled_high = scaled.astype(BF)
    scaled_low = (scaled - scaled_high.astype(F32)).astype(BF)
    grad_coef = dot(relation_hot, scaled_high, 1, 1) + dot(relation_hot, scaled_low, 1, 1)
    coef_total = lax.psum(grad_coef, ("dom", "feat"))
    return (
        output,
        grad_feats,
        whole[:cut].reshape(basis_count, quarter, width),
        whole[cut:].T,
        coef_total * scale,
    )


def solution(mesh):
    return jax.shard_map(
        body,
        mesh=mesh,
        in_specs=(
            P("feat", "dom"),
            P(None, "feat"),
            P(None, "feat", None),
            P(),
            P("dom", None),
            P("dom"),
            P("dom"),
            P("dom"),
            P("dom", None),
            P("dom", None),
            P("feat", "dom"),
        ),
        out_specs=(P("feat", "dom"), P("feat", "dom"), P(None, "feat", None), P(None, "feat"), P()),
        check_vma=False,
    )
```

time: 307 us -> 254 us (0.83)
  blocking collectives: 54.4 us -> 188 us
  waiting for transfers between devices: 59.7 us -> 6.93 us
  local copies, waits for them, and re-layouts: 62.4 us -> 12.2 us
  other arithmetic: 57.8 us -> 13.7 us
  starting transfers between devices: 36.3 us -> 7.11 us
  between operations: 16 us -> 0.91 us
  matrix products: 18.1 us -> 24.1 us
    all_gather x2 -> x4, blocking collectives: 13.2 us -> 107 us  [the longest x1 33.2 us: body(): table = lax.all_gather(feats, 'dom', axis=1, tiled=True)]
    psum x1 -> x0, waiting for transfers between devices: 51.5 us -> none  [body(): bases_total, self_total = lax.psum((grad_bases, self_term), 'dom')]
    scatter-add x3 -> x0, other arithmetic: 37.8 us -> none  [the longest x1 14.7 us: body(): jnp.zeros((entities,), jnp.float32).at[arriving].add(1.0, mode='drop')]
    all_to_all x0 -> x2, blocking collectives: none -> 37.6 us  [the longest x1 23.6 us: scatter_sum(): lax.all_to_all(values, axis, split_axis=1, concat_axis=0, tiled=True)]
    gather x8 -> x0, local copies, waits for them, and re-layouts: 31.3 us -> none  [the longest x2 13.2 us: body(): jnp.take(inverse_degree, arriving, mode='fill', fill_value=0.0)[None]]
    all_to_all x6 -> x2, starting transfers between devices: 36 us -> 7.11 us  [the longest x1 3.62 us: body(): lax.all_to_all(stacked, 'dom', split_axis=0, concat_axis=0, tiled=True)]
    scatter x4 -> x0, local copies, waits for them, and re-layouts: 9.47 us -> none  [the longest x1 5.04 us: body(): jnp.full((dom_count * slot_cap,), entities, jnp.int32).at[slot_index]]
    dot_general x0 -> x1, local copies, waits for them, and re-layouts: none -> 9.08 us  [dot(): lax.dot_general(left, right, (((left_axis,), (right_axis,)), ((), ())), p...]
  transfers between devices with their start and end apart: 9 -> 2, of which waited for: 2 -> 1; matrix products, arithmetic and copies ran while one was open for 18% -> 4% of each run, Pallas kernels for 0% -> 0%
where the time goes in v1:
time: 254 us; the launch traced here: 253 us
  blocking collectives  188 us (74%)
  matrix products  24.1 us (9%)
  other arithmetic  13.7 us (5%)
  local copies, waits for them, and re-layouts  12.2 us (5%)
  starting transfers between devices  7.11 us (3%)
  waiting for transfers between devices  6.93 us (3%)
    psum x1, blocking collectives, body(): coef_total = lax.psum(grad_coef, ('dom', 'feat'))  44.3 us
    all_gather x1, blocking collectives, body(): table = lax.all_gather(feats, 'dom', axis=1, tiled=True)  33.2 us
    all_gather x1, blocking collectives, body(): lax.all_gather(piece.astype(BF), 'dom', axis=0, tiled=True).astype(F32)  32.9 us
    all_gather x1, blocking collectives, body(): grad_table = lax.all_gather(grad_node, 'dom', axis=1, tiled=True)  31.8 us
    dot_general x15, matrix products, dot(): lax.dot_general(left, right, (((left_axis,), (right_axis,)), ((), ())), p...  24.1 us
    all_to_all x1, blocking collectives, scatter_sum(): lax.all_to_all(values, axis, split_axis=1, concat_axis=0, tiled=True)  23.6 us
    all_to_all x1, blocking collectives, body(): both = lax.all_to_all(both, 'feat', split_axis=0, concat_axis=0, tiled=True)  14 us
    dot_general x1, local copies, waits for them, and re-layouts, dot(): lax.dot_general(left, right, (((left_axis,), (right_axis,)), ((), ())), p...  9.08 us
  transfers between devices with their start and end apart: 2, of which 1 were waited for; matrix products, arithmetic and copies ran while one was open for 4% of the time, Pallas kernels for 0%

profile of v1, /device:TPU:0, one launch (start us, length us, event | category | flops | bytes accessed | tf_op | source)
XLA Modules:
  0.0 253.4 jit_solution(16554198673092056434)
XLA Ops:
  0.6 0.0 copy-start
  0.7 1.2 fusion.18
  1.8 1.1 fusion.19
  2.9 0.7 broadcast_multiply_fusion.1
  3.6 33.2 %all_gather.12 = bf16[64,4096]{1,0:T(8,128)(2,1)S(1)} all-gather(bf16[64,512]{1,0:T(8,128)(2,1)} %param.13), channel_id=1, replica_groups=mesh['dom'=8,'feat'=4] {'dom'}, dimensions={1}, use_global_device_ids=true | all-gather | bytes 589824 | tf_op jit(solution)/shard_map/all_gather | solution.py:83
  36.9 0.7 add.36
  37.5 2.8 %fusion.13 = bf16[64,1024]{1,0:T(8,128)(2,1)S(1)} fusion(bf16[64,4096]{1,0:T(8,128)(2,1)S(1)} %all_gather.12, s32[1024]{0:T(1024)S(1)} %add.36), kind=kOutput, calls=%fused_computation.25 | convolution fusion | flops 541130752 | bytes 659456 | tf_op jit(solution)/shard_map/dot_general | solution.py:11
  40.3 8.6 %all_gather.13 = bf16[256,1536]{1,0:T(8,128)(2,1)S(1)} all-gather(bf16[64,1536]{1,0:T(8,128)(2,1)S(1)} %pad_maximum_fusion.2), channel_id=1, replica_groups=mesh['dom'=8,'feat'=4] {'feat'}, dimensions={0}, use_global_device_ids=true | all-gather | bytes 983040 | tf_op jit(solution)/shard_map/all_gather | solution.py:85
  49.0 4.5 %convolution_bitcast_fusion = f32[1920,1024]{0,1:T(8,128)} fusion(bf16[1920,256]{1,0:T(8,128)(2,1)S(1)} %bitcast.63, bf16[256,1536]{1,0:T(8,128)(2,1)S(1)} %all_gather.13), kind=kOutput, calls=%fused_computation.14 | convolution fusion | flops 1006632960 | bytes 9371648 | tf_op jit(solution)/shard_map/dot_general | solution.py:11
  53.4 9.1 %copy.19 = f32[1920,1024]{1,0:T(8,128)} copy(f32[1920,1024]{0,1:T(8,128)} %convolution_bitcast_fusion) | data formatting | bytes 15728640 | tf_op jit(solution)/shard_map/dot_general | solution.py:11
  62.6 0.0 copy-start.9
  62.6 0.3 fusion.15
  62.9 4.1 %multiply_reduce_fusion.1 = bf16[64,1024]{1,0:T(8,128)(2,1)S(1)} fusion(f32[30,64,1024]{2,1,0:T(8,128)} %bitcast.64, f32[30,1024]{1,0:T(8,128)S(1)} %fusion.15), kind=kLoop, calls=%fused_computation.12 | loop fusion | flops 3866624 | bytes 8118272 | tf_op jit(solution)/shard_map/reduce_sum | solution.py:101
  67.0 0.1 fusion.39
  67.1 3.4 %fusion.1 = f32[80,4096]{1,0:T(8,128)S(1)} fusion(s32[1024]{0:T(1024)S(1)} %fusion.39, bf16[16,1024]{1,0:T(8,128)(2,1)S(1)} %copy-done.9, bf16[64,1024]{1,0:T(8,128)(2,1)S(1)} %multiply_reduce_fusion.1), kind=kOutput, calls=%fused_computation.2 | convolution fusion | flops 675610624 | bytes 1478656 | tf_op jit(solution)/shard_map/dot_general | solution.py:11
  70.5 0.1 slice.101
  70.7 0.1 pad.9.clone
  70.7 0.2 maximum_maximum_fusion
  71.0 23.6 %all_to_all.35 = bf16[80,8,512]{2,0,1:T(8,128)(2,1)S(1)} all-to-all(bf16[80,8,512]{2,0,1:T(8,128)(2,1)S(1)} %maximum_maximum_fusion), channel_id=1, replica_groups=mesh['dom'=8,'feat'=4] {'dom'}, dimensions={1} | all-to-all | bytes 1310720 | tf_op jit(solution)/shard_map/all_to_all | solution.py:48
  94.6 0.1 convert_reduce_fusion.2
  94.7 0.9 multiply_convert_fusion.3
  95.6 31.8 %all_gather.14 = bf16[64,4096]{1,0:T(8,128)(2,1)S(1)} all-gather(bf16[64,512]{1,0:T(8,128)(2,1)S(1)} %get-tuple-element.17), channel_id=1, replica_groups=mesh['dom'=8,'feat'=4] {'dom'}, dimensions={1}, use_global_device_ids=true | all-gather | bytes 589824 | tf_op jit(solution)/shard_map/all_gather | solution.py:123
  127.4 3.2 %fusion.12 = f32[64,1024]{1,0:T(8,128)S(1)} fusion(bf16[64,4096]{1,0:T(8,128)(2,1)S(1)} %all_gather.14, s32[1024]{0:T(1024)S(1)} %fusion.39), kind=kOutput, calls=%fused_computation.24 | convolution fusion | flops 541196288 | bytes 790528 | tf_op jit(solution)/shard_map/dot_general | solution.py:11
  130.6 1.3 fusion.9
  131.9 0.3 convolution_convert_fusion.1
  132.1 0.1 pad_maximum_fusion.1
  132.2 14.0 %all_to_all.36 = bf16[4,64,1536]{2,1,0:T(8,128)(2,1)S(1)} all-to-all(bf16[4,64,1536]{2,1,0:T(8,128)(2,1)S(1)} %pad_maximum_fusion.1), channel_id=1, replica_groups=mesh['dom'=8,'feat'=4] {'feat'}, dimensions={0} | all-to-all | bytes 1572864 | tf_op jit(solution)/shard_map/all_to_all | solution.py:135
  146.2 0.1 convert_reduce_fusion.1
  146.4 3.4 %fusion.8 = bf16[64,4096]{1,0:T(8,128)(2,1)S(1)} fusion(s32[1024]{0:T(1024)S(1)} %add.36, f32[64,1536]{1,0:T(8,128)S(1)} %convert_reduce_fusion.1), kind=kOutput, calls=%fused_computation.13 | convolution fusion | flops 541327360 | bytes 659456 | tf_op jit(solution)/shard_map/dot_general | solution.py:11
  149.7 0.9 copy.28
  150.6 3.5 %all-to-all-start.2 = ((bf16[64,8,512]{2,0,1:T(8,128)(2,1)}), bf16[64,8,512]{2,0,1:T(8,128)(2,1)S(1)}, u32[]{:S(2)}, u32[]{:S(2)}) async-start(bf16[64,8,512]{2,0,1:T(8,128)(2,1)} %bitcast.61), calls=%async_computation.2 | async-start | bytes 1048576 | tf_op jit(solution)/shard_map/all_to_all | solution.py:48
  154.1 4.9 %multiply_reduce_fusion = (f32[30,1024]{1,0:T(8,128)S(1)}, bf16[30,64,1024]{2,1,0:T(8,128)(2,1)S(1)}) fusion(f32[30,64,1024]{2,1,0:T(8,128)} %bitcast.65, f32[64,1024]{1,0:T(8,128)S(1)} %fusion.12, f32[30,1024]{1,0:T(8,128)S(1)} %fusion.15), kind=kLoop, calls=%fused_computation.10 | loop fusion | flops 7833600 | bytes 12304384 | tf_op jit(solution)/shard_map/reduce_sum | solution.py:127
  159.0 0.2 convolution_convert_fusion.2
  159.2 1.3 convolution_convert_fusion
  160.5 1.0 pad_maximum_fusion
  161.5 6.9 %all-to-all-done.2 = bf16[64,8,512]{2,0,1:T(8,128)(2,1)S(1)} async-done(((bf16[64,8,512]{2,0,1:T(8,128)(2,1)}), bf16[64,8,512]{2,0,1:T(8,128)(2,1)S(1)}, u32[]{:S(2)}, u32[]{:S(2)}) %all-to-all-start.2) | async-done | bytes 524320 | tf_op jit(solution)/shard_map/all_to_all | solution.py:48
  168.4 3.6 %all-to-all-start.3 = ((bf16[8,248,256]{2,1,0:T(8,128)(2,1)}), bf16[8,248,256]{2,1,0:T(8,128)(2,1)S(1)}, u32[]{:S(2)}, u32[]{:S(2)}) async-start(bf16[8,248,256]{2,1,0:T(8,128)(2,1)} %bitcast.20), calls=%async_computation.3 | async-start | bytes 2031616 | tf_op jit(solution)/shard_map/all_to_all | solution.py:143
  172.0 0.3 fusion.17
  172.3 0.3 convolution_add_fusion
  172.6 44.3 %psum.7 = f32[237,30]{0,1:T(8,128)S(1)} all-reduce(f32[237,30]{0,1:T(8,128)S(1)} %convolution_add_fusion), channel_id=1, replica_groups=mesh['dom'=8,'feat'=4] {'dom','feat'}, use_global_device_ids=true, to_apply=%region_6.7 | all-reduce | flops 7110 | bytes 56880 | tf_op jit(solution)/shard_map/psum | solution.py:151
  216.8 0.6 broadcast_multiply_fusion
  217.5 0.1 convert_reduce_fusion.3
  217.5 0.7 fusion.32
  218.2 0.1 convert_reduce_fusion
  218.4 32.9 %all_gather.15 = bf16[1984,256]{1,0:T(8,128)(2,1)S(1)} all-gather(bf16[248,256]{1,0:T(8,128)(2,1)S(1)} %multiply_convert_fusion.2), channel_id=1, replica_groups=mesh['dom'=8,'feat'=4] {'dom'}, dimensions={0}, use_global_device_ids=true | all-gather | bytes 1142784 | tf_op jit(solution)/shard_map/all_gather | solution.py:145
  251.2 0.2 convert_element_type.128
  251.4 1.4 slice.69
  252.8 0.6 slice_bitcast_fusion
  (26 shorter events, 0.2 us)
Async XLA Ops:
  0.6 48.3 %copy-start = (bf16[30,64,256]{2,1,0:T(8,128)(2,1)S(1)}, bf16[30,64,256]{2,1,0:T(8,128)(2,1)}, u32[]{:S(2)}) copy-start(bf16[30,64,256]{2,1,0:T(8,128)(2,1)} %param.15) | copy-start | bytes 2949124
  0.6 39.7 %copy-start.1 = (bf16[64,512]{1,0:T(8,128)(2,1)S(1)}, bf16[64,512]{1,0:T(8,128)(2,1)}, u32[]{:S(2)}) copy-start(bf16[64,512]{1,0:T(8,128)(2,1)} %param.13) | copy-start | bytes 196612
  53.4 9.1 %copy-start.8 = (s32[8,1]{0,1:T(1,128)S(1)}, s32[8,1]{0,1:T(1,128)}, u32[]{:S(2)}) copy-start(s32[8,1]{0,1:T(1,128)} %param.21) | copy-start | bytes 100
  53.4 9.1 %copy-start.2 = (f32[237,30]{0,1:T(8,128)S(1)}, f32[237,30]{0,1:T(8,128)}, u32[]{:S(2)}) copy-start(f32[237,30]{0,1:T(8,128)} %param.16) | copy-start | bytes 85324
  53.4 9.1 %copy-start.4 = (s32[1024]{0:T(1024)S(1)}, s32[1024]{0:T(1024)}, u32[]{:S(2)}) copy-start(s32[1024]{0:T(1024)} %param.20) | copy-start | bytes 12292
  62.5 4.5 %copy-start.5 = (s32[1024]{0:T(1024)S(1)}, s32[1024]{0:T(1024)}, u32[]{:S(2)}) copy-start(s32[1024]{0:T(1024)} %param.19) | copy-start | bytes 12292
  62.6 4.5 %copy-start.6 = (s32[1,8]{1,0:T(1,128)S(1)}, s32[1,8]{1,0:T(1,128)}, u32[]{:S(2)}) copy-start(s32[1,8]{1,0:T(1,128)} %param.22) | copy-start | bytes 100
  62.6 4.5 %copy-start.9 = (bf16[16,1024]{1,0:T(8,128)(2,1)S(1)}, bf16[16,1024]{1,0:T(8,128)(2,1)}, u32[]{:S(2)}) copy-start(bf16[16,1024]{1,0:T(8,128)(2,1)} %constant.47.clone.1) | copy-start | bytes 98308
  70.5 24.2 %copy-start.3 = (bf16[256,64]{0,1:T(8,128)(2,1)S(1)}, bf16[256,64]{0,1:T(8,128)(2,1)}, u32[]{:S(2)}) copy-start(bf16[256,64]{0,1:T(8,128)(2,1)} %param.14) | copy-start | bytes 98308
  70.5 24.2 %copy-start.7 = (bf16[64,512]{1,0:T(8,128)(2,1)S(1)}, bf16[64,512]{1,0:T(8,128)(2,1)}, u32[]{:S(2)}) copy-start(bf16[64,512]{1,0:T(8,128)(2,1)} %param.23) | copy-start | bytes 196612
  150.6 17.8 %all-to-all-start.2 = ((bf16[64,8,512]{2,0,1:T(8,128)(2,1)}), bf16[64,8,512]{2,0,1:T(8,128)(2,1)S(1)}, u32[]{:S(2)}, u32[]{:S(2)}) async-start(bf16[64,8,512]{2,0,1:T(8,128)(2,1)} %bitcast.61), calls=%async_computation.2 | async-start | bytes 1048576 | tf_op jit(solution)/shard_map/all_to_all | solution.py:48
  168.4 49.8 %all-to-all-start.3 = ((bf16[8,248,256]{2,1,0:T(8,128)(2,1)}), bf16[8,248,256]{2,1,0:T(8,128)(2,1)S(1)}, u32[]{:S(2)}, u32[]{:S(2)}) async-start(bf16[8,248,256]{2,1,0:T(8,128)(2,1)} %bitcast.20), calls=%async_computation.3 | async-start | bytes 2031616 | tf_op jit(solution)/shard_map/all_to_all | solution.py:143

commit v2 on v1

v2 whole, which is shorter than its diff:
```python
import functools

import jax
import jax.numpy as jnp
from jax import lax
from jax.experimental import pallas as pl
from jax.experimental.pallas import tpu as pltpu
from jax.sharding import PartitionSpec as P

BF = jnp.bfloat16
F32 = jnp.float32


def dot(left, right, left_axis, right_axis):
    return lax.dot_general(
        left, right, (((left_axis,), (right_axis,)), ((), ())), preferred_element_type=F32
    )


def onehot(ids, start, size):
    return (jnp.arange(size, dtype=jnp.int32)[:, None] + start == ids[None, :]).astype(BF)


def pick(table, ids, chunk):
    width = table.shape[1]
    if width <= chunk:
        return dot(table, onehot(ids, 0, width), 1, 0).astype(BF)

    def step(index, total):
        piece = lax.dynamic_slice_in_dim(table, index * chunk, chunk, 1)
        return total + dot(piece, onehot(ids, index * chunk, chunk), 1, 0)

    total = lax.fori_loop(
        0, width // chunk, step, jnp.zeros((table.shape[0], ids.shape[0]), F32)
    )
    return total.astype(BF)


def spread(values, ids, width, chunk):
    if width <= chunk:
        return dot(values, onehot(ids, 0, width), 1, 1)

    def step(index, total):
        piece = dot(values, onehot(ids, index * chunk, chunk), 1, 1)
        return lax.dynamic_update_slice_in_dim(total, piece, index * chunk, 1)

    return lax.fori_loop(0, width // chunk, step, jnp.zeros((values.shape[0], width), F32))


def peers(axis, count):
    me = lax.axis_index(axis)
    return me, me // 2, me % 2, count // 2


def greet(axis, me, spot, side, columns):
    barrier = pltpu.get_barrier_semaphore()
    pl.semaphore_signal(
        barrier, inc=1, device_id={axis: spot * 2 + 1 - side}, device_id_type=pl.DeviceIdType.MESH
    )
    for hop in range(1, columns):
        other = (spot + hop) % columns
        pl.semaphore_signal(
            barrier, inc=1, device_id={axis: other * 2 + side}, device_id_type=pl.DeviceIdType.MESH
        )
    pl.semaphore_wait(barrier, columns)


def gather_kernel(axis, count, x_ref, o_ref, own_sem, send, recv, pair_send, pair_recv):
    me, spot, side, columns = peers(axis, count)
    mate = spot * 2 + 1 - side
    greet(axis, me, spot, side, columns)

    def remote(source, place, send_sem, recv_sem, target):
        return pltpu.make_async_remote_copy(
            src_ref=source,
            dst_ref=o_ref.at[place],
            send_sem=send_sem,
            recv_sem=recv_sem,
            device_id={axis: target},
            device_id_type=pl.DeviceIdType.MESH,
        )

    started = []
    for hop in range(1, columns):
        target = (spot + hop) % columns * 2 + side
        copy = remote(x_ref, me, send.at[hop - 1], recv.at[hop - 1], target)
        copy.start()
        started.append(copy)
    first = remote(x_ref, me, pair_send.at[0], pair_recv.at[0], mate)
    first.start()
    own = pltpu.make_async_copy(x_ref, o_ref.at[me], own_sem)
    own.start()
    passed = [first]
    for hop in range(1, columns):
        started[hop - 1].wait_recv()
        place = (spot - hop + columns) % columns * 2 + side
        copy = remote(o_ref.at[place], place, pair_send.at[hop], pair_recv.at[hop], mate)
        copy.start()
        passed.append(copy)
    own.wait()
    for copy in started:
        copy.wait_send()
    for copy in passed:
        copy.wait()


def all_gather(values, axis, count, ident):
    columns = count // 2
    return pl.pallas_call(
        functools.partial(gather_kernel, axis, count),
        out_shape=jax.ShapeDtypeStruct((count,) + values.shape, values.dtype),
        in_specs=[pl.BlockSpec(memory_space=pltpu.VMEM)],
        out_specs=pl.BlockSpec(memory_space=pltpu.VMEM),
        scratch_shapes=[
            pltpu.SemaphoreType.DMA,
            pltpu.SemaphoreType.DMA((columns - 1,)),
            pltpu.SemaphoreType.DMA((columns - 1,)),
            pltpu.SemaphoreType.DMA((columns,)),
            pltpu.SemaphoreType.DMA((columns,)),
        ],
        compiler_params=pltpu.CompilerParams(collective_id=ident, has_side_effects=True),
    )(values)


def reduce_kernel(
    axis, count, x_ref, o_ref, landed, summed, arrived, send, recv, pair_send, pair_recv
):
    me, spot, side, columns = peers(axis, count)
    mate = spot * 2 + 1 - side
    greet(axis, me, spot, side, columns)
    order = [(spot + hop) % columns for hop in list(range(1, columns)) + [0]]
    passed = []
    for step, place in enumerate(order):
        copy = pltpu.make_async_remote_copy(
            src_ref=x_ref.at[place * 2 + 1 - side],
            dst_ref=landed.at[step],
            send_sem=pair_send.at[step],
            recv_sem=pair_recv.at[step],
            device_id={axis: mate},
            device_id_type=pl.DeviceIdType.MESH,
        )
        copy.start()
        passed.append(copy)
    started = []
    for step, place in enumerate(order):
        passed[step].wait_recv()
        total = x_ref[place * 2 + side].astype(F32) + landed[step].astype(F32)
        summed[step] = total.astype(BF)
        if step < columns - 1:
            copy = pltpu.make_async_remote_copy(
                src_ref=summed.at[step],
                dst_ref=arrived.at[step],
                send_sem=send.at[step],
                recv_sem=recv.at[step],
                device_id={axis: place * 2 + side},
                device_id_type=pl.DeviceIdType.MESH,
            )
            copy.start()
            started.append(copy)
    total = summed[columns - 1].astype(F32)
    for step, copy in enumerate(started):
        copy.wait_recv()
        total = total + arrived[step].astype(F32)
    o_ref[...] = total
    for copy in started + passed:
        copy.wait_send()


def reduce_parts(values, axis, count, ident):
    columns = count // 2
    shape = values.shape[1:]
    return pl.pallas_call(
        functools.partial(reduce_kernel, axis, count),
        out_shape=jax.ShapeDtypeStruct(shape, F32),
        in_specs=[pl.BlockSpec(memory_space=pltpu.VMEM)],
        out_specs=pl.BlockSpec(memory_space=pltpu.VMEM),
        scratch_shapes=[
            pltpu.VMEM((columns,) + shape, BF),
            pltpu.VMEM((columns,) + shape, BF),
            pltpu.VMEM((columns - 1,) + shape, BF),
            pltpu.SemaphoreType.DMA((columns - 1,)),
            pltpu.SemaphoreType.DMA((columns - 1,)),
            pltpu.SemaphoreType.DMA((columns,)),
            pltpu.SemaphoreType.DMA((columns,)),
        ],
        compiler_params=pltpu.CompilerParams(collective_id=ident, has_side_effects=True),
    )(values)


def by_part(values, count):
    rows, columns = values.shape
    return values.reshape(rows, count, columns // count).transpose(1, 0, 2)


def side_by_side(parts):
    count, rows, columns = parts.shape
    return parts.transpose(1, 0, 2).reshape(rows, count * columns)


def group_of(count):
    return max(size for size in range(1, 6) if count % size == 0)


def forward_kernel(group, bases_ref, sources_ref, weights_ref, out_ref):
    basis_count, quarter, width = bases_ref.shape
    sources = sources_ref[...]

    def step(index, total):
        part = bases_ref[pl.ds(index * group, group)].reshape(group * quarter, width)
        products = jnp.dot(part, sources, preferred_element_type=F32)
        for k in range(group):
            weight = weights_ref[pl.ds(index * group + k, 1), :]
            total = total + products[k * quarter:(k + 1) * quarter] * weight
        return total

    total = lax.fori_loop(0, basis_count // group, step, jnp.zeros(out_ref.shape, F32))
    out_ref[...] = total.astype(BF)


def backward_kernel(
    group, bases_ref, sources_ref, weights_ref, grad_ref, bases_out, scaled_out, edge_out
):
    basis_count, quarter, width = bases_ref.shape
    sources = sources_ref[...]
    edge_out[...] = jnp.zeros(edge_out.shape, F32)

    def step(index, carry):
        part = bases_ref[pl.ds(index * group, group)].reshape(group * quarter, width)
        products = jnp.dot(part, sources, preferred_element_type=F32)
        grad = grad_ref[...].astype(F32)
        combined = []
        for k in range(group):
            spot = pl.ds(index * group + k, 1)
            scaled_out[spot, :] = jnp.sum(
                products[k * quarter:(k + 1) * quarter] * grad, axis=0, keepdims=True
            )
            combined.append((grad * weights_ref[spot, :]).astype(BF))
        combined = jnp.concatenate(combined, axis=0)
        piece = dot(combined, sources, 1, 1)
        bases_out[pl.ds(index * group, group)] = piece.reshape(group, quarter, width).astype(BF)
        edge_out[...] += dot(part, combined, 0, 0)
        return carry

    lax.fori_loop(0, basis_count // group, step, 0)


def body(
    feats,
    self_weight,
    bases,
    coef,
    src_part,
    src_row,
    edge_dst,
    edge_rel,
    block_owner,
    block_valid,
    cotangent,
):
    dom_count = lax.axis_size("dom")
    feat_count = lax.axis_size("feat")
    quarter, entities = feats.shape
    edge_count = src_row.shape[0]
    block_count = block_valid.shape[1]
    block_rows = edge_count // block_count
    basis_count, _, width = bases.shape
    relations = coef.shape[0]
    total_entities = dom_count * entities
    chunk = min(8, dom_count) * entities
    scale = float(edge_count * dom_count) ** (-0.5)

    source_ids = src_part[:, 0] * entities + src_row
    live = (jnp.arange(block_rows)[None, :] < block_valid[0][:, None]).reshape(edge_count)
    owners = jnp.broadcast_to(block_owner, (block_count, block_rows)).reshape(edge_count)
    target_ids = jnp.where(live, owners * entities + edge_dst, -1)
    relation_hot = onehot(edge_rel, 0, relations)

    table = side_by_side(all_gather(feats, "dom", dom_count, 0))
    source_quarter = pick(table, source_ids, chunk)
    gathered = all_gather(
        jnp.concatenate([source_quarter, feats], axis=1), "feat", feat_count, 1
    ).reshape(width, edge_count + entities)
    sources = gathered[:, :edge_count]
    own_full = gathered[:, edge_count:]

    group = group_of(basis_count)
    vmem = pl.BlockSpec(memory_space=pltpu.VMEM)
    first = coef.astype(BF)
    second = (coef - first.astype(F32)).astype(BF)
    third = (coef - first.astype(F32) - second.astype(F32)).astype(BF)
    weights = (
        dot(first, relation_hot, 0, 0)
        + dot(second, relation_hot, 0, 0)
        + dot(third, relation_hot, 0, 0)
    )
    messages = pl.pallas_call(
        functools.partial(forward_kernel, group),
        out_shape=jax.ShapeDtypeStruct((quarter, edge_count), BF),
        in_specs=[vmem] * 3,
        out_specs=vmem,
    )(bases, sources, weights)
    extra = 16
    tail = jnp.zeros((extra, edge_count), BF).at[0].set(1.0)
    partial = spread(jnp.concatenate([messages, tail], axis=0), target_ids, total_entities, chunk)
    counted = partial[quarter:quarter + 1]
    high = jnp.floor(counted / 64.0)
    counts = jnp.concatenate(
        [high, counted - 64.0 * high, jnp.zeros((extra - 2, total_entities), F32)], axis=0
    )
    sent = jnp.concatenate([partial[:quarter], counts], axis=0).astype(BF)
    arrived = reduce_parts(by_part(sent, dom_count), "dom", dom_count, 2)
    aggregate = arrived[:quarter]
    degree = arrived[quarter:quarter + 1] * 64.0 + arrived[quarter + 1:quarter + 2]
    inverse_degree = 1.0 / jnp.maximum(degree, 1.0)
    preact = dot(self_weight, own_full, 0, 0) + inverse_degree * aggregate
    output = jax.nn.silu(preact).astype(BF)
    sigmoid_pre = jax.nn.sigmoid(preact)
    grad_pre = (
        cotangent.astype(F32) * sigmoid_pre * (1.0 + preact * (1.0 - sigmoid_pre))
    ).astype(BF)
    grad_node = (grad_pre.astype(F32) * inverse_degree).astype(BF)
    grad_table = side_by_side(all_gather(grad_node, "dom", dom_count, 3))
    grad_message = pick(grad_table, target_ids, chunk)

    grad_bases, scaled, edge_partial = pl.pallas_call(
        functools.partial(backward_kernel, group),
        out_shape=(
            jax.ShapeDtypeStruct((basis_count, quarter, width), BF),
            jax.ShapeDtypeStruct((basis_count, edge_count), F32),
            jax.ShapeDtypeStruct((width, edge_count), F32),
        ),
        in_specs=[vmem] * 4,
        out_specs=(vmem,) * 3,
    )(bases, sources, weights, grad_message)
    self_partial = dot(self_weight, grad_pre, 1, 0)
    self_term = dot(grad_pre, own_full, 1, 1)

    scaled_high = scaled.astype(BF)
    scaled_low = (scaled - scaled_high.astype(F32)).astype(BF)
    grad_coef = dot(scaled_high, relation_hot, 1, 1) + dot(scaled_low, relation_hot, 1, 1)
    lanes = -(-relations // 256) * 256
    coef_size = -(-basis_count // 32) * 32 * lanes
    coef_wide = coef_size // quarter
    padded = jnp.pad(
        grad_coef, ((0, coef_size // lanes - basis_count), (0, lanes - relations))
    ).reshape(quarter, coef_wide)
    both = jnp.concatenate([edge_partial, self_partial], axis=1).reshape(feat_count, quarter, -1)
    spare = jnp.broadcast_to(padded[None], (feat_count, quarter, coef_wide))
    both = jnp.concatenate([both, spare], axis=2).astype(BF)
    both = reduce_parts(both, "feat", feat_count, 4)
    edge_grads = both[:, :edge_count].astype(BF)
    self_grads = both[:, edge_count:edge_count + entities]
    coef_sum = both[:, edge_count + entities:].reshape(-1, width).astype(BF)
    node_grads = by_part(
        spread(edge_grads, source_ids, total_entities, chunk).astype(BF), dom_count
    )

    cut = basis_count * quarter
    rows = cut + quarter + coef_sum.shape[0]
    more = -rows % (16 * dom_count)
    stacked = jnp.concatenate(
        [
            grad_bases.reshape(cut, width),
            self_term.astype(BF),
            coef_sum,
            jnp.zeros((more, width), BF),
        ],
        axis=0,
    ).reshape(dom_count, -1, width)
    height = stacked.shape[1]
    reduced = reduce_parts(
        jnp.concatenate([stacked, node_grads.reshape(dom_count, -1, width)], axis=1),
        "dom",
        dom_count,
        5,
    )
    grad_feats = (self_grads + reduced[height:].reshape(quarter, entities)).astype(BF)
    piece = (reduced[:height] * scale).astype(BF)
    whole = all_gather(piece, "dom", dom_count, 6).reshape(-1, width).astype(F32)
    coef_total = whole[cut + quarter:cut + quarter + coef_sum.shape[0]]
    coef_total = coef_total.reshape(-1, lanes)[:basis_count, :relations].T
    return (
        output,
        grad_feats,
        whole[:cut].reshape(basis_count, quarter, width),
        whole[cut:cut + quarter].T,
        coef_total,
    )


def solution(mesh):
    return jax.shard_map(
        body,
        mesh=mesh,
        in_specs=(
            P("feat", "dom"),
            P(None, "feat"),
            P(None, "feat", None),
            P(),
            P("dom", None),
            P("dom"),
            P("dom"),
            P("dom"),
            P("dom", None),
            P("dom", None),
            P("feat", "dom"),
        ),
        out_specs=(P("feat", "dom"), P("feat", "dom"), P(None, "feat", None), P(None, "feat"), P()),
        check_vma=False,
    )
```

time: 254 us -> 175 us (0.69)
  blocking collectives: 188 us -> 0 us
  Pallas kernels: 0 us -> 129 us
  starting transfers between devices: 7.11 us -> 0 us
  waiting for transfers between devices: 6.93 us -> 0 us
  local copies, waits for them, and re-layouts: 12.2 us -> 8.21 us
  matrix products: 24.1 us -> 20.9 us
    pallas_call x0 -> x9, Pallas kernels: none -> 129 us  [the longest x4 62.2 us: all_gather(): pl.pallas_call(functools.partial(gather_kernel, axis, count), out_shape=j...]
    all_gather x4 -> x0, blocking collectives: 107 us -> none  [the longest x1 33.2 us: body(): table = lax.all_gather(feats, 'dom', axis=1, tiled=True)]
    psum x1 -> x0, blocking collectives: 44.3 us -> none  [body(): coef_total = lax.psum(grad_coef, ('dom', 'feat'))]
    all_to_all x2 -> x0, blocking collectives: 37.6 us -> none  [the longest x1 23.6 us: scatter_sum(): lax.all_to_all(values, axis, split_axis=1, concat_axis=0, tiled=True)]
    reduce_sum x6 -> x0, other arithmetic: 9.43 us -> none  [the longest x1 4.88 us: body(): scaled = jnp.sum(products * grad_float[None], axis=1)]
    dot_general x1 -> x0, local copies, waits for them, and re-layouts: 9.08 us -> none  [dot(): lax.dot_general(left, right, (((left_axis,), (right_axis,)), ((), ())), p...]
    all_to_all x2 -> x0, starting transfers between devices: 7.11 us -> none  [the longest x1 3.62 us: body(): lax.all_to_all(stacked, 'dom', split_axis=0, concat_axis=0, tiled=True)]
    all_to_all x2 -> x0, waiting for transfers between devices: 6.93 us -> none  [the longest x1 6.93 us: scatter_sum(): lax.all_to_all(values, axis, split_axis=1, concat_axis=0, tiled=True)]
  transfers between devices with their start and end apart: 2 -> 0, of which waited for: 1 -> 0; matrix products, arithmetic and copies ran while one was open for 4% -> 0% of each run, Pallas kernels for 0% -> 0%
where the time goes in v2:
time: 175 us; the launch traced here: 174 us
  Pallas kernels  129 us (74%)
  matrix products  20.9 us (12%)
  other arithmetic  14.9 us (9%)
  local copies, waits for them, and re-layouts  8.21 us (5%)
    pallas_call x4, Pallas kernels, all_gather(): pl.pallas_call(functools.partial(gather_kernel, axis, count), out_shape=j...  62.2 us
    pallas_call x3, Pallas kernels, reduce_parts(): pl.pallas_call(functools.partial(reduce_kernel, axis, count), out_shape=j...  54.8 us
    dot_general x12, matrix products, dot(): lax.dot_general(left, right, (((left_axis,), (right_axis,)), ((), ())), p...  20.9 us
    pallas_call x1, Pallas kernels, body(): pl.pallas_call(functools.partial(backward_kernel, group), out_shape=(jax....  7.51 us
    pallas_call x1, Pallas kernels, body(): pl.pallas_call(functools.partial(forward_kernel, group), out_shape=jax.Sh...  4.23 us

profile of v2, /device:TPU:0, one launch (start us, length us, event | category | flops | bytes accessed | tf_op | source)
XLA Modules:
  0.0 173.7 jit_solution(4198639736834615440)
XLA Ops:
  0.6 0.7 multiply_bitcast_fusion
  1.3 0.1 pad.20.clone
  1.4 0.8 fusion.36
  2.2 0.1 pad.12.clone
  2.2 0.7 broadcast_multiply_fusion
  2.9 0.7 add.36
  3.6 1.1 fusion.17
  4.7 1.1 fusion.18
  5.8 1.7 fusion.14.weights_ref
  7.6 17.2 %shard_map.146 = bf16[8,64,512]{2,1,0:T(8,128)(2,1)} custom-call(bf16[64,512]{1,0:T(8,128)(2,1)} %x_ref.1), custom_call_target="tpu_custom_call" | custom-call | tf_op jit(solution)/shard_map/pallas_call | solution.py:109
  24.7 1.1 copy.26
  25.8 2.8 %fusion.12 = bf16[64,1024]{1,0:T(8,128)(2,1)S(1)} fusion(bf16[64,4096]{1,0:T(8,128)(2,1)S(1)} %bitcast.80, s32[1024]{0:T(1024)S(1)} %add.36), kind=kOutput, calls=%fused_computation.16 | convolution fusion | flops 541130752 | bytes 659456 | tf_op jit(solution)/shard_map/dot_general | solution.py:15
  28.6 0.7 pad_maximum_fusion.3.x_ref
  29.3 10.0 %shard_map.147 = bf16[4,64,1536]{2,1,0:T(8,128)(2,1)} custom-call(bf16[64,1536]{1,0:T(8,128)(2,1)} %pad_maximum_fusion.3.x_ref), custom_call_target="tpu_custom_call" | custom-call | tf_op jit(solution)/shard_map/pallas_call | solution.py:109
  39.3 1.9 %slice.80.sources_ref = bf16[256,1024]{1,0:T(8,128)(2,1)} slice(bf16[256,1536]{1,0:T(8,128)(2,1)} %bitcast.68), slice={[0:256], [0:1024]} | slice | bytes 1048576 | tf_op jit(solution)/shard_map/slice | solution.py:283
  41.2 4.2 %shard_map.148 = bf16[64,1024]{1,0:T(8,128)(2,1)} custom-call(bf16[30,64,256]{2,1,0:T(8,128)(2,1)} %bases_ref.3, bf16[256,1024]{1,0:T(8,128)(2,1)} %slice.80.sources_ref, f32[30,1024]{1,0:T(8,128)} %fusion.14.weights_ref), custom_call_target="tpu_custom_call" | custom-call | tf_op jit(solution)/shard_map/pallas_call | solution.py:296
  45.4 4.3 %fusion.1 = f32[80,4096]{1,0:T(8,128)S(1)} fusion(s32[1024]{0:T(1024)S(1)} %fusion.36, bf16[16,1024]{1,0:T(8,128)(2,1)S(1)} %copy-done.7, bf16[64,1024]{1,0:T(8,128)(2,1)} %shard_map.148), kind=kOutput, calls=%fused_computation.2 | convolution fusion | flops 675610624 | bytes 1478656 | tf_op jit(solution)/shard_map/dot_general | solution.py:15
  49.8 0.1 slice.104
  49.9 1.1 maximum_bitcast_fusion.x_ref
  50.9 16.2 %shard_map.149 = f32[80,512]{1,0:T(8,128)} custom-call(bf16[8,80,512]{2,1,0:T(8,128)(2,1)} %maximum_bitcast_fusion.x_ref), custom_call_target="tpu_custom_call" | custom-call | tf_op jit(solution)/shard_map/pallas_call | solution.py:172
  67.2 0.8 maximum_divide_fusion
  68.0 1.8 %multiply_convert_fusion.1 = (bf16[64,512]{1,0:T(8,128)(2,1)}, bf16[64,512]{1,0:T(8,128)(2,1)S(1)}, bf16[64,512]{1,0:T(8,128)(2,1)}) fusion(f32[512]{0:T(512)S(1)} %bitcast.84, bf16[64,512]{1,0:T(8,128)(2,1)S(1)} %copy-done.6, f32[80,512]{1,0:T(8,128)} %shard_map.149, bf16[256,64]{0,1:T(8,128)(2,1)S(1)} %copy-done, bf16[256,1536]{1,0:T(8,128)(2,1)S(1)} %bitcast.69), kind=kOutput, calls=%fused_computation.51 | convolution fusion | flops 17334272 | bytes 690176 | tf_op jit(solution)/shard_map/dot_general | solution.py:15
  69.8 0.2 convolution_convert_fusion.1
  70.0 0.3 fusion.9
  70.3 14.4 %shard_map.150 = bf16[8,64,512]{2,1,0:T(8,128)(2,1)} custom-call(bf16[64,512]{1,0:T(8,128)(2,1)} %get-tuple-element.23.x_ref), custom_call_target="tpu_custom_call" | custom-call | tf_op jit(solution)/shard_map/pallas_call | solution.py:109
  84.6 1.1 copy.27
  85.7 3.8 %fusion.11.grad_ref = bf16[64,1024]{1,0:T(8,128)(2,1)} fusion(bf16[64,4096]{1,0:T(8,128)(2,1)S(1)} %bitcast.78, s32[1024]{0:T(1024)S(1)} %fusion.36), kind=kOutput, calls=%fused_computation.15 | convolution fusion | flops 541130752 | bytes 659456 | tf_op jit(solution)/shard_map/dot_general | solution.py:15
  89.6 7.5 %shard_map.151 = (bf16[30,64,256]{2,1,0:T(8,128)(2,1)}, f32[30,1024]{1,0:T(8,128)}, f32[256,1024]{1,0:T(8,128)}) custom-call(bf16[30,64,256]{2,1,0:T(8,128)(2,1)} %bases_ref.3, bf16[256,1024]{1,0:T(8,128)(2,1)} %slice.80.sources_ref, f32[30,1024]{1,0:T(8,128)} %fusion.14.weights_ref, bf16[64,1024]{1,0:T(8,128)(2,1)} %fusion.11.grad_ref), custom_call_target="tpu_custom_call" | custom-call | tf_op jit(solution)/shard_map/pallas_call | solution.py:325
  97.1 1.3 convert.36
  98.4 0.1 pad_maximum_fusion.2
  98.5 0.3 fusion.16
  98.8 0.3 convolution_add_fusion
  99.1 1.0 pad_maximum_fusion.1.x_ref
  100.1 9.4 %shard_map.152 = f32[64,1664]{1,0:T(8,128)} custom-call(bf16[4,64,1664]{2,1,0:T(8,128)(2,1)} %pad_maximum_fusion.1.x_ref), custom_call_target="tpu_custom_call" | custom-call | tf_op jit(solution)/shard_map/pallas_call | solution.py:172
  109.5 1.0 convert.39
  110.6 0.3 maximum_maximum_fusion
  111.0 3.3 %fusion.8 = bf16[64,4096]{1,0:T(8,128)(2,1)S(1)} fusion(s32[1024]{0:T(1024)S(1)} %add.36, bf16[64,1664]{1,0:T(8,128)(2,1)S(1)} %convert.39), kind=kOutput, calls=%fused_computation.10 | convolution fusion | flops 541327360 | bytes 659456 | tf_op jit(solution)/shard_map/dot_general | solution.py:15
  114.3 0.2 reshape.99
  114.5 1.3 pad_maximum_fusion.x_ref
  115.7 29.1 %shard_map.153 = f32[384,256]{1,0:T(8,128)} custom-call(bf16[8,384,256]{2,1,0:T(8,128)(2,1)} %pad_maximum_fusion.x_ref), custom_call_target="tpu_custom_call" | custom-call | tf_op jit(solution)/shard_map/pallas_call | solution.py:172
  144.9 1.6 multiply_convert_fusion.x_ref
  146.5 0.9 slice.74
  147.4 1.6 add_convert_fusion
  149.0 20.7 %shard_map.154 = bf16[8,256,256]{2,1,0:T(8,128)(2,1)} custom-call(bf16[256,256]{1,0:T(8,128)(2,1)} %multiply_convert_fusion.x_ref), custom_call_target="tpu_custom_call" | custom-call | tf_op jit(solution)/shard_map/pallas_call | solution.py:109
  169.7 1.4 bitcast_convert_fusion
  171.1 0.6 slice_bitcast_fusion.1
  171.7 0.6 slice_bitcast_fusion
  172.3 1.4 slice.85
  (27 shorter events, 0.3 us)
Async XLA Ops:
  0.6 67.3 %copy-start = (bf16[256,64]{0,1:T(8,128)(2,1)S(1)}, bf16[256,64]{0,1:T(8,128)(2,1)}, u32[]{:S(2)}) copy-start(bf16[256,64]{0,1:T(8,128)(2,1)} %param.14) | copy-start | bytes 98308
  25.8 2.8 %copy-start.3 = (bf16[64,512]{1,0:T(8,128)(2,1)S(1)}, bf16[64,512]{1,0:T(8,128)(2,1)}, u32[]{:S(2)}) copy-start(bf16[64,512]{1,0:T(8,128)(2,1)} %x_ref.1) | copy-start | bytes 196612
  28.6 16.9 %copy-start.7 = (bf16[16,1024]{1,0:T(8,128)(2,1)S(1)}, bf16[16,1024]{1,0:T(8,128)(2,1)}, u32[]{:S(2)}) copy-start(bf16[16,1024]{1,0:T(8,128)(2,1)} %constant.47.clone.1) | copy-start | bytes 98308
  49.7 18.3 %copy-start.1 = (bf16[4,64,1536]{2,1,0:T(8,128)(2,1)S(1)}, bf16[4,64,1536]{2,1,0:T(8,128)(2,1)}, u32[]{:S(2)}) copy-start(bf16[4,64,1536]{2,1,0:T(8,128)(2,1)} %shard_map.147) | copy-start | bytes 2359300
  49.7 18.3 %copy-start.6 = (bf16[64,512]{1,0:T(8,128)(2,1)S(1)}, bf16[64,512]{1,0:T(8,128)(2,1)}, u32[]{:S(2)}) copy-start(bf16[64,512]{1,0:T(8,128)(2,1)} %param.23) | copy-start | bytes 196612
  89.6 8.9 %copy-start.4 = (s32[1024]{0:T(1024)S(1)}, s32[1024]{0:T(1024)}, u32[]{:S(2)}) copy-start(s32[1024]{0:T(1024)} %param.20) | copy-start | bytes 12292
  97.1 1.4 copy-start.5
  98.8 11.8 %copy-start.2 = (bf16[30,64,256]{2,1,0:T(8,128)(2,1)S(1)}, bf16[30,64,256]{2,1,0:T(8,128)(2,1)}, u32[]{:S(2)}) copy-start(bf16[30,64,256]{2,1,0:T(8,128)(2,1)} %get-tuple-element.22) | copy-start | bytes 2949124

commit v3 on v1

v3 whole, which is shorter than its diff:
```python
import functools

import jax
import jax.numpy as jnp
from jax import lax
from jax.experimental import pallas as pl
from jax.experimental.pallas import tpu as pltpu
from jax.sharding import PartitionSpec as P

BF = jnp.bfloat16
F32 = jnp.float32


def dot(left, right, left_axis, right_axis):
    return lax.dot_general(
        left, right, (((left_axis,), (right_axis,)), ((), ())), preferred_element_type=F32
    )


def onehot(ids, start, size):
    return (jnp.arange(size, dtype=jnp.int32)[:, None] + start == ids[None, :]).astype(BF)


def spread(values, ids, width, chunk):
    if width <= chunk:
        return dot(values, onehot(ids, 0, width), 1, 1)

    def step(index, total):
        piece = dot(values, onehot(ids, index * chunk, chunk), 1, 1)
        return lax.dynamic_update_slice_in_dim(total, piece, index * chunk, 1)

    return lax.fori_loop(0, width // chunk, step, jnp.zeros((values.shape[0], width), F32))


def peers(axis, count):
    me = lax.axis_index(axis)
    return me, me // 2, me % 2, count // 2


def greet(groups):
    barrier = pltpu.get_barrier_semaphore()
    expected = 0
    for axis, count in groups:
        me, spot, side, columns = peers(axis, count)
        targets = [spot * 2 + 1 - side]
        targets += [(spot + hop) % columns * 2 + side for hop in range(1, columns)]
        for target in targets:
            pl.semaphore_signal(
                barrier, inc=1, device_id={axis: target}, device_id_type=pl.DeviceIdType.MESH
            )
        expected += columns
    pl.semaphore_wait(barrier, expected)


def remote(source, target_ref, send_sem, recv_sem, axis, target):
    return pltpu.make_async_remote_copy(
        src_ref=source,
        dst_ref=target_ref,
        send_sem=send_sem,
        recv_sem=recv_sem,
        device_id={axis: target},
        device_id_type=pl.DeviceIdType.MESH,
    )


class Gather:
    def __init__(self, axis, count, x_ref, o_ref, own_sem, send, recv, pair_send, pair_recv):
        self.me, self.spot, self.side, self.columns = peers(axis, count)
        self.axis, self.o_ref = axis, o_ref
        self.mate = self.spot * 2 + 1 - self.side
        self.pair_send, self.pair_recv = pair_send, pair_recv
        self.started, self.passed = [], []
        for hop in range(1, self.columns):
            target = (self.spot + hop) % self.columns * 2 + self.side
            copy = remote(
                x_ref, o_ref.at[self.me], send.at[hop - 1], recv.at[hop - 1], axis, target
            )
            copy.start()
            self.started.append(copy)
        first = remote(
            x_ref, o_ref.at[self.me], pair_send.at[0], pair_recv.at[0], axis, self.mate
        )
        first.start()
        self.passed.append(first)
        self.own = pltpu.make_async_copy(x_ref, o_ref.at[self.me], own_sem)
        self.own.start()

    def place(self, hop, side):
        return (self.spot - hop + self.columns) % self.columns * 2 + side

    def forward(self, hop):
        self.started[hop - 1].wait_recv()
        place = self.place(hop, self.side)
        copy = remote(
            self.o_ref.at[place],
            self.o_ref.at[place],
            self.pair_send.at[hop],
            self.pair_recv.at[hop],
            self.axis,
            self.mate,
        )
        copy.start()
        self.passed.append(copy)
        return place

    def from_mate(self, hop):
        self.passed[hop].wait_recv()
        return self.place(hop, 1 - self.side)

    def finish(self):
        for copy in self.started + self.passed:
            copy.wait_send()


def gather_scratch(count):
    columns = count // 2
    return [
        pltpu.SemaphoreType.DMA,
        pltpu.SemaphoreType.DMA((columns - 1,)),
        pltpu.SemaphoreType.DMA((columns - 1,)),
        pltpu.SemaphoreType.DMA((columns,)),
        pltpu.SemaphoreType.DMA((columns,)),
    ]


class Reduce:
    def __init__(
        self, axis, count, x_ref, landed, summed, arrived, send, recv, pair_send, pair_recv
    ):
        me, spot, side, columns = peers(axis, count)
        self.axis, self.side, self.columns, self.x_ref = axis, side, columns, x_ref
        self.landed, self.summed, self.arrived = landed, summed, arrived
        self.send, self.recv = send, recv
        self.order = [(spot + hop) % columns for hop in list(range(1, columns)) + [0]]
        self.passed, self.started = [], []
        for step, place in enumerate(self.order):
            copy = remote(
                x_ref.at[place * 2 + 1 - side],
                landed.at[step],
                pair_send.at[step],
                pair_recv.at[step],
                axis,
                spot * 2 + 1 - side,
            )
            copy.start()
            self.passed.append(copy)

    def middle(self, step):
        place = self.order[step]
        self.passed[step].wait_recv()
        total = self.x_ref[place * 2 + self.side].astype(F32) + self.landed[step].astype(F32)
        self.summed[step] = total.astype(BF)
        if step < self.columns - 1:
            copy = remote(
                self.summed.at[step],
                self.arrived.at[step],
                self.send.at[step],
                self.recv.at[step],
                self.axis,
                place * 2 + self.side,
            )
            copy.start()
            self.started.append(copy)

    def finish(self, o_ref):
        total = self.summed[self.columns - 1].astype(F32)
        for step, copy in enumerate(self.started):
            copy.wait_recv()
            total = total + self.arrived[step].astype(F32)
        o_ref[...] = total
        for copy in self.started + self.passed:
            copy.wait_send()


def reduce_scratch(count, shape):
    columns = count // 2
    return [
        pltpu.VMEM((columns,) + shape, BF),
        pltpu.VMEM((columns,) + shape, BF),
        pltpu.VMEM((columns - 1,) + shape, BF),
        pltpu.SemaphoreType.DMA((columns - 1,)),
        pltpu.SemaphoreType.DMA((columns - 1,)),
        pltpu.SemaphoreType.DMA((columns,)),
        pltpu.SemaphoreType.DMA((columns,)),
    ]


def exchange(kernel, out_shape, args, scratch, ident):
    vmem = pl.BlockSpec(memory_space=pltpu.VMEM)
    return pl.pallas_call(
        kernel,
        out_shape=out_shape,
        in_specs=[vmem] * len(args),
        out_specs=jax.tree.map(lambda leaf: vmem, out_shape),
        scratch_shapes=scratch,
        compiler_params=pltpu.CompilerParams(collective_id=ident, has_side_effects=True),
    )(*args)


def all_gather(values, axis, count, ident):
    def kernel(x_ref, o_ref, *scratch):
        greet([(axis, count)])
        gather = Gather(axis, count, x_ref, o_ref, *scratch)
        for hop in range(1, gather.columns):
            gather.forward(hop)
        gather.own.wait()
        for hop in range(gather.columns):
            gather.from_mate(hop)
        gather.finish()

    shape = jax.ShapeDtypeStruct((count,) + values.shape, values.dtype)
    return exchange(kernel, shape, (values,), gather_scratch(count), ident)


def gather_pick(values, ids, axis, count, ident):
    def kernel(x_ref, ids_ref, o_ref, table, total, *scratch):
        extent = x_ref.shape[1]
        greet([(axis, count)])
        gather = Gather(axis, count, x_ref, table, *scratch)
        rows = lax.broadcasted_iota(jnp.int32, (extent, ids_ref.shape[1]), 0)

        def use(place):
            hot = jnp.where(rows + place * extent == ids_ref[...], 1.0, 0.0).astype(BF)
            total[...] += jnp.dot(table[place], hot, preferred_element_type=F32)

        total[...] = jnp.zeros(total.shape, F32)
        gather.own.wait()
        use(gather.me)
        for hop in range(1, gather.columns):
            use(gather.forward(hop))
        for hop in range(gather.columns):
            use(gather.from_mate(hop))
        o_ref[...] = total[...].astype(BF)
        gather.finish()

    shape = (values.shape[0], ids.shape[1])
    scratch = [pltpu.VMEM((count,) + values.shape, BF), pltpu.VMEM(shape, F32)]
    return exchange(
        kernel,
        jax.ShapeDtypeStruct(shape, BF),
        (values, ids),
        scratch + gather_scratch(count),
        ident,
    )


def reduce_parts(values, axis, count, ident):
    def kernel(x_ref, o_ref, *scratch):
        greet([(axis, count)])
        reduce = Reduce(axis, count, x_ref, *scratch)
        for step in range(reduce.columns):
            reduce.middle(step)
        reduce.finish(o_ref)

    shape = values.shape[1:]
    return exchange(
        kernel, jax.ShapeDtypeStruct(shape, F32), (values,), reduce_scratch(count, shape), ident
    )


def reduce_both(first, axis, count, second, other_axis, other_count, ident):
    def kernel(x_ref, y_ref, o_ref, p_ref, *scratch):
        greet([(axis, count), (other_axis, other_count)])
        short = Reduce(axis, count, x_ref, *scratch[:7])
        long = Reduce(other_axis, other_count, y_ref, *scratch[7:])
        for step in range(short.columns):
            short.middle(step)
        for step in range(long.columns):
            long.middle(step)
        short.finish(o_ref)
        long.finish(p_ref)

    shape, other = first.shape[1:], second.shape[1:]
    return exchange(
        kernel,
        (jax.ShapeDtypeStruct(shape, F32), jax.ShapeDtypeStruct(other, F32)),
        (first, second),
        reduce_scratch(count, shape) + reduce_scratch(other_count, other),
        ident,
    )


def reduce_gather(values, pieces, axis, count, ident):
    def kernel(x_ref, y_ref, o_ref, p_ref, *scratch):
        greet([(axis, count)])
        reduce = Reduce(axis, count, x_ref, *scratch[:7])
        gather = Gather(axis, count, y_ref, p_ref, *scratch[7:])
        for step in range(reduce.columns):
            reduce.middle(step)
        for hop in range(1, gather.columns):
            gather.forward(hop)
        gather.own.wait()
        reduce.finish(o_ref)
        for hop in range(gather.columns):
            gather.from_mate(hop)
        gather.finish()

    shape = values.shape[1:]
    return exchange(
        kernel,
        (
            jax.ShapeDtypeStruct(shape, F32),
            jax.ShapeDtypeStruct((count,) + pieces.shape, pieces.dtype),
        ),
        (values, pieces),
        reduce_scratch(count, shape) + gather_scratch(count),
        ident,
    )


def by_part(values, count):
    rows, columns = values.shape
    return values.reshape(rows, count, columns // count).transpose(1, 0, 2)


def group_of(count):
    return max(size for size in range(1, 6) if count % size == 0)


def forward_kernel(group, bases_ref, sources_ref, weights_ref, out_ref):
    basis_count, quarter, width = bases_ref.shape
    sources = sources_ref[...]

    def step(index, total):
        part = bases_ref[pl.ds(index * group, group)].reshape(group * quarter, width)
        products = jnp.dot(part, sources, preferred_element_type=F32)
        for k in range(group):
            weight = weights_ref[pl.ds(index * group + k, 1), :]
            total = total + products[k * quarter:(k + 1) * quarter] * weight
        return total

    total = lax.fori_loop(0, basis_count // group, step, jnp.zeros(out_ref.shape, F32))
    out_ref[...] = total.astype(BF)


def backward_kernel(
    group, bases_ref, sources_ref, weights_ref, grad_ref, bases_out, scaled_out, edge_out
):
    basis_count, quarter, width = bases_ref.shape
    sources = sources_ref[...]
    edge_out[...] = jnp.zeros(edge_out.shape, F32)

    def step(index, carry):
        part = bases_ref[pl.ds(index * group, group)].reshape(group * quarter, width)
        products = jnp.dot(part, sources, preferred_element_type=F32)
        grad = grad_ref[...].astype(F32)
        combined = []
        for k in range(group):
            spot = pl.ds(index * group + k, 1)
            scaled_out[spot, :] = jnp.sum(
                products[k * quarter:(k + 1) * quarter] * grad, axis=0, keepdims=True
            )
            combined.append((grad * weights_ref[spot, :]).astype(BF))
        combined = jnp.concatenate(combined, axis=0)
        piece = dot(combined, sources, 1, 1)
        bases_out[pl.ds(index * group, group)] = piece.reshape(group, quarter, width).astype(BF)
        edge_out[...] += dot(part, combined, 0, 0)
        return carry

    lax.fori_loop(0, basis_count // group, step, 0)


def body(
    feats,
    self_weight,
    bases,
    coef,
    src_part,
    src_row,
    edge_dst,
    edge_rel,
    block_owner,
    block_valid,
    cotangent,
):
    dom_count = lax.axis_size("dom")
    feat_count = lax.axis_size("feat")
    quarter, entities = feats.shape
    edge_count = src_row.shape[0]
    block_count = block_valid.shape[1]
    block_rows = edge_count // block_count
    basis_count, _, width = bases.shape
    relations = coef.shape[0]
    total_entities = dom_count * entities
    chunk = min(8, dom_count) * entities
    scale = float(edge_count * dom_count) ** (-0.5)

    source_ids = src_part[:, 0] * entities + src_row
    live = (jnp.arange(block_rows)[None, :] < block_valid[0][:, None]).reshape(edge_count)
    owners = jnp.broadcast_to(block_owner, (block_count, block_rows)).reshape(edge_count)
    target_ids = jnp.where(live, owners * entities + edge_dst, -1)
    relation_hot = onehot(edge_rel, 0, relations)

    source_quarter = gather_pick(feats, source_ids[None, :], "dom", dom_count, 0)
    gathered = all_gather(
        jnp.concatenate([source_quarter, feats], axis=1), "feat", feat_count, 1
    ).reshape(width, edge_count + entities)
    sources = gathered[:, :edge_count]
    own_full = gathered[:, edge_count:]

    group = group_of(basis_count)
    vmem = pl.BlockSpec(memory_space=pltpu.VMEM)
    first = coef.astype(BF)
    second = (coef - first.astype(F32)).astype(BF)
    third = (coef - first.astype(F32) - second.astype(F32)).astype(BF)
    weights = (
        dot(first, relation_hot, 0, 0)
        + dot(second, relation_hot, 0, 0)
        + dot(third, relation_hot, 0, 0)
    )
    messages = pl.pallas_call(
        functools.partial(forward_kernel, group),
        out_shape=jax.ShapeDtypeStruct((quarter, edge_count), BF),
        in_specs=[vmem] * 3,
        out_specs=vmem,
    )(bases, sources, weights)
    extra = 16
    tail = jnp.zeros((extra, edge_count), BF).at[0].set(1.0)
    partial = spread(jnp.concatenate([messages, tail], axis=0), target_ids, total_entities, chunk)
    counted = partial[quarter:quarter + 1]
    high = jnp.floor(counted / 64.0)
    counts = jnp.concatenate(
        [high, counted - 64.0 * high, jnp.zeros((extra - 2, total_entities), F32)], axis=0
    )
    sent = jnp.concatenate([partial[:quarter], counts], axis=0).astype(BF)
    arrived = reduce_parts(by_part(sent, dom_count), "dom", dom_count, 2)
    aggregate = arrived[:quarter]
    degree = arrived[quarter:quarter + 1] * 64.0 + arrived[quarter + 1:quarter + 2]
    inverse_degree = 1.0 / jnp.maximum(degree, 1.0)
    preact = dot(self_weight, own_full, 0, 0) + inverse_degree * aggregate
    output = jax.nn.silu(preact).astype(BF)
    sigmoid_pre = jax.nn.sigmoid(preact)
    grad_pre = (
        cotangent.astype(F32) * sigmoid_pre * (1.0 + preact * (1.0 - sigmoid_pre))
    ).astype(BF)
    grad_node = (grad_pre.astype(F32) * inverse_degree).astype(BF)
    grad_message = gather_pick(grad_node, target_ids[None, :], "dom", dom_count, 3)

    grad_bases, scaled, edge_partial = pl.pallas_call(
        functools.partial(backward_kernel, group),
        out_shape=(
            jax.ShapeDtypeStruct((basis_count, quarter, width), BF),
            jax.ShapeDtypeStruct((basis_count, edge_count), F32),
            jax.ShapeDtypeStruct((width, edge_count), F32),
        ),
        in_specs=[vmem] * 4,
        out_specs=(vmem,) * 3,
    )(bases, sources, weights, grad_message)
    self_partial = dot(self_weight, grad_pre, 1, 0)
    self_term = dot(grad_pre, own_full, 1, 1)

    scaled_high = scaled.astype(BF)
    scaled_low = (scaled - scaled_high.astype(F32)).astype(BF)
    grad_coef = dot(scaled_high, relation_hot, 1, 1) + dot(scaled_low, relation_hot, 1, 1)
    lanes = -(-relations // 256) * 256
    coef_size = -(-basis_count // 32) * 32 * lanes
    coef_wide = coef_size // quarter
    padded = jnp.pad(
        grad_coef, ((0, coef_size // lanes - basis_count), (0, lanes - relations))
    ).reshape(quarter, coef_wide)
    both = jnp.concatenate([edge_partial, self_partial], axis=1).reshape(feat_count, quarter, -1)
    spare = jnp.broadcast_to(padded[None], (feat_count, quarter, coef_wide))
    both = jnp.concatenate([both, spare], axis=2).astype(BF)
    cut = basis_count * quarter
    more = -(cut + quarter) % (16 * dom_count)
    stacked = jnp.concatenate(
        [grad_bases.reshape(cut, width), self_term.astype(BF), jnp.zeros((more, width), BF)],
        axis=0,
    ).reshape(dom_count, -1, width)
    both, piece = reduce_both(both, "feat", feat_count, stacked, "dom", dom_count, 4)
    edge_grads = both[:, :edge_count].astype(BF)
    self_grads = both[:, edge_count:edge_count + entities]
    coef_sum = both[:, edge_count + entities:].reshape(-1, width)
    node_grads = by_part(
        spread(edge_grads, source_ids, total_entities, chunk).astype(BF), dom_count
    )
    height = piece.shape[0]
    pieces = (jnp.concatenate([piece, coef_sum], axis=0) * scale).astype(BF)
    node_sum, gathered = reduce_gather(node_grads, pieces, "dom", dom_count, 5)
    grad_feats = (self_grads + node_sum).astype(BF)
    whole = gathered[:, :height].reshape(-1, width).astype(F32)
    coef_total = jnp.sum(gathered[:, height:].astype(F32), axis=0)
    coef_total = coef_total.reshape(-1, lanes)[:basis_count, :relations].T
    return (
        output,
        grad_feats,
        whole[:cut].reshape(basis_count, quarter, width),
        whole[cut:cut + quarter].T,
        coef_total,
    )


def solution(mesh):
    return jax.shard_map(
        body,
        mesh=mesh,
        in_specs=(
            P("feat", "dom"),
            P(None, "feat"),
            P(None, "feat", None),
            P(),
            P("dom", None),
            P("dom"),
            P("dom"),
            P("dom"),
            P("dom", None),
            P("dom", None),
            P("feat", "dom"),
        ),
        out_specs=(P("feat", "dom"), P("feat", "dom"), P(None, "feat", None), P(None, "feat"), P()),
        check_vma=False,
    )
```

time: 254 us -> 153 us (0.60)
  blocking collectives: 188 us -> 0 us
  Pallas kernels: 0 us -> 111 us
  matrix products: 24.1 us -> 15.3 us
  starting transfers between devices: 7.11 us -> 0 us
  waiting for transfers between devices: 6.93 us -> 0 us
  local copies, waits for them, and re-layouts: 12.2 us -> 7.84 us
    pallas_call x0 -> x8, Pallas kernels: none -> 111 us  [the longest x6 99.6 us: exchange(): pl.pallas_call(kernel, out_shape=out_shape, in_specs=[vmem] * len(args),...]
    all_gather x4 -> x0, blocking collectives: 107 us -> none  [the longest x1 33.2 us: body(): table = lax.all_gather(feats, 'dom', axis=1, tiled=True)]
    psum x1 -> x0, blocking collectives: 44.3 us -> none  [body(): coef_total = lax.psum(grad_coef, ('dom', 'feat'))]
    all_to_all x2 -> x0, blocking collectives: 37.6 us -> none  [the longest x1 23.6 us: scatter_sum(): lax.all_to_all(values, axis, split_axis=1, concat_axis=0, tiled=True)]
    dot_general x1 -> x0, local copies, waits for them, and re-layouts: 9.08 us -> none  [dot(): lax.dot_general(left, right, (((left_axis,), (right_axis,)), ((), ())), p...]
    dot_general x15 -> x10, matrix products: 24.1 us -> 15.3 us  [dot(): lax.dot_general(left, right, (((left_axis,), (right_axis,)), ((), ())), p...]
    reduce_sum x6 -> x1, other arithmetic: 9.43 us -> 0.93 us  [body(): coef_total = jnp.sum(gathered[:, height:].astype(F32), axis=0)]
    all_to_all x2 -> x0, starting transfers between devices: 7.11 us -> none  [the longest x1 3.62 us: body(): lax.all_to_all(stacked, 'dom', split_axis=0, concat_axis=0, tiled=True)]
  transfers between devices with their start and end apart: 2 -> 0, of which waited for: 1 -> 0; matrix products, arithmetic and copies ran while one was open for 4% -> 0% of each run, Pallas kernels for 0% -> 0%
where the time goes in v3:
time: 153 us; the launch traced here: 150 us
  Pallas kernels  111 us (73%)
  matrix products  15.3 us (10%)
  other arithmetic  15.1 us (10%)
  local copies, waits for them, and re-layouts  7.84 us (5%)
    pallas_call x6, Pallas kernels, exchange(): pl.pallas_call(kernel, out_shape=out_shape, in_specs=[vmem] * len(args),...  99.6 us
    dot_general x10, matrix products, dot(): lax.dot_general(left, right, (((left_axis,), (right_axis,)), ((), ())), p...  15.3 us
    pallas_call x1, Pallas kernels, body(): pl.pallas_call(functools.partial(backward_kernel, group), out_shape=(jax....  7.51 us
    pallas_call x1, Pallas kernels, body(): pl.pallas_call(functools.partial(forward_kernel, group), out_shape=jax.Sh...  4.24 us

profile of v3, /device:TPU:0, one launch (start us, length us, event | category | flops | bytes accessed | tf_op | source)
XLA Modules:
  0.0 150.4 jit_solution(1946928633393800426)
XLA Ops:
  0.6 0.0 copy-start
  0.6 0.7 multiply_bitcast_fusion
  1.3 0.1 pad.19.clone
  1.4 0.8 fusion.29
  2.2 0.1 pad.11.clone
  2.2 0.7 broadcast_multiply_fusion
  2.9 1.3 add.36
  4.2 17.3 %shard_map.146 = bf16[64,1024]{1,0:T(8,128)(2,1)} custom-call(bf16[64,512]{1,0:T(8,128)(2,1)} %x_ref.1, s32[1,1024]{1,0:T(1,128)} %bitcast.71), custom_call_target="tpu_custom_call" | custom-call | tf_op jit(solution)/shard_map/pallas_call | solution.py:190
  21.5 1.6 %pad_maximum_fusion.2.x_ref = bf16[64,1536]{1,0:T(8,128)(2,1)} fusion(bf16[64,512]{1,0:T(8,128)(2,1)} %x_ref.1, bf16[64,1024]{1,0:T(8,128)(2,1)} %shard_map.146), kind=kLoop, calls=%fused_computation.39 | loop fusion | flops 393216 | bytes 393216 | tf_op jit(solution)/shard_map/concatenate | solution.py:396
  23.2 1.1 fusion.10
  24.3 1.1 fusion.11
  25.4 1.7 %fusion.7.weights_ref = f32[30,1024]{1,0:T(8,128)} fusion(f32[30,1024]{1,0:T(8,128)S(1)} %fusion.10, f32[30,1024]{1,0:T(8,128)S(1)} %fusion.11, s32[1024]{0:T(1024)} %param.20, f32[237,30]{0,1:T(8,128)} %param.16), kind=kOutput, calls=%fused_computation.12 | convolution fusion | flops 14872518 | bytes 401176 | tf_op jit(solution)/shard_map/dot_general | solution.py:15
  27.1 10.0 %shard_map.147 = bf16[4,64,1536]{2,1,0:T(8,128)(2,1)} custom-call(bf16[64,1536]{1,0:T(8,128)(2,1)} %pad_maximum_fusion.2.x_ref), custom_call_target="tpu_custom_call" | custom-call | tf_op jit(solution)/shard_map/pallas_call | solution.py:190
  37.2 1.9 %slice.77.sources_ref = bf16[256,1024]{1,0:T(8,128)(2,1)} slice(bf16[256,1536]{1,0:T(8,128)(2,1)} %bitcast.60), slice={[0:256], [0:1024]} | slice | bytes 1048576 | tf_op jit(solution)/shard_map/slice | solution.py:398
  39.1 4.2 %shard_map.148 = bf16[64,1024]{1,0:T(8,128)(2,1)} custom-call(bf16[30,64,256]{2,1,0:T(8,128)(2,1)} %bases_ref.3, bf16[256,1024]{1,0:T(8,128)(2,1)} %slice.77.sources_ref, f32[30,1024]{1,0:T(8,128)} %fusion.7.weights_ref), custom_call_target="tpu_custom_call" | custom-call | tf_op jit(solution)/shard_map/pallas_call | solution.py:411
  43.3 4.3 %fusion = f32[80,4096]{1,0:T(8,128)S(1)} fusion(s32[1024]{0:T(1024)S(1)} %fusion.29, bf16[16,1024]{1,0:T(8,128)(2,1)S(1)} %copy-done.8, bf16[64,1024]{1,0:T(8,128)(2,1)} %shard_map.148), kind=kOutput, calls=%fused_computation.2 | convolution fusion | flops 675610624 | bytes 1478656 | tf_op jit(solution)/shard_map/dot_general | solution.py:15
  47.6 0.1 slice.100
  47.7 0.0 copy-start.7
  47.7 1.1 maximum_bitcast_fusion.x_ref
  48.8 16.2 %shard_map.149 = f32[80,512]{1,0:T(8,128)} custom-call(bf16[8,80,512]{2,1,0:T(8,128)(2,1)} %maximum_bitcast_fusion.x_ref), custom_call_target="tpu_custom_call" | custom-call | tf_op jit(solution)/shard_map/pallas_call | solution.py:190
  65.0 0.8 maximum_divide_fusion
  65.9 1.8 %multiply_convert_fusion = (bf16[64,512]{1,0:T(8,128)(2,1)}, bf16[64,512]{1,0:T(8,128)(2,1)S(1)}, bf16[64,512]{1,0:T(8,128)(2,1)}) fusion(f32[512]{0:T(512)S(1)} %bitcast.74, bf16[64,512]{1,0:T(8,128)(2,1)S(1)} %copy-done.7, f32[80,512]{1,0:T(8,128)} %shard_map.149, bf16[256,64]{0,1:T(8,128)(2,1)S(1)} %copy-done, bf16[256,1536]{1,0:T(8,128)(2,1)S(1)} %bitcast.61), kind=kOutput, calls=%fused_computation.45 | convolution fusion | flops 17334272 | bytes 690176 | tf_op jit(solution)/shard_map/dot_general | solution.py:15
  67.7 0.2 convolution_convert_fusion.1
  67.9 14.5 %shard_map.150.grad_ref = bf16[64,1024]{1,0:T(8,128)(2,1)} custom-call(bf16[64,512]{1,0:T(8,128)(2,1)} %get-tuple-element.31.x_ref, s32[1,1024]{1,0:T(1,128)} %bitcast.72), custom_call_target="tpu_custom_call" | custom-call | tf_op jit(solution)/shard_map/pallas_call | solution.py:190
  82.4 0.3 fusion.5
  82.7 7.5 %shard_map.151 = (bf16[30,64,256]{2,1,0:T(8,128)(2,1)}, f32[30,1024]{1,0:T(8,128)}, f32[256,1024]{1,0:T(8,128)}) custom-call(bf16[30,64,256]{2,1,0:T(8,128)(2,1)} %bases_ref.3, bf16[256,1024]{1,0:T(8,128)(2,1)} %slice.77.sources_ref, f32[30,1024]{1,0:T(8,128)} %fusion.7.weights_ref, bf16[64,1024]{1,0:T(8,128)(2,1)} %shard_map.150.grad_ref), custom_call_target="tpu_custom_call" | custom-call | tf_op jit(solution)/shard_map/pallas_call | solution.py:439
  90.2 1.4 convert.35
  91.6 0.0 copy-start.5
  91.6 0.1 pad_maximum_fusion.1
  91.7 0.0 copy-done.2
  91.7 1.3 maximum_maximum_fusion
  93.0 0.3 fusion.9
  93.3 0.3 convolution_add_fusion
  93.6 0.0 copy-start.3
  93.6 1.0 pad_maximum_fusion.x_ref
  94.6 19.2 %shard_map.152 = (f32[64,1664]{1,0:T(8,128)}, f32[256,256]{1,0:T(8,128)}) custom-call(bf16[4,64,1664]{2,1,0:T(8,128)(2,1)} %pad_maximum_fusion.x_ref, bf16[8,256,256]{2,1,0:T(8,128)(2,1)} %bitcast.58), custom_call_target="tpu_custom_call" | custom-call | tf_op jit(solution)/shard_map/pallas_call | solution.py:190
  113.9 0.8 slice.70
  114.6 1.6 %fusion.17.y_ref = bf16[288,256]{1,0:T(8,128)(2,1)} fusion(f32[32,256]{1,0:T(8,128)S(1)} %reshape.86, f32[256,256]{1,0:T(8,128)} %get-tuple-element.28), kind=kLoop, calls=%fused_computation.34 | loop fusion | flops 221184 | bytes 442368 | tf_op jit(solution)/shard_map/convert_element_type | solution.py:478
  116.3 4.3 %fusion.4 = bf16[64,4096]{1,0:T(8,128)(2,1)S(1)} fusion(s32[1024]{0:T(1024)S(1)} %copy-done.3, f32[64,1664]{1,0:T(8,128)} %get-tuple-element.27), kind=kOutput, calls=%fused_computation.6 | convolution fusion | flops 541327360 | bytes 659456 | tf_op jit(solution)/shard_map/dot_general | solution.py:15
  120.6 0.8 copy.25
  121.4 22.2 %shard_map.153 = (f32[64,512]{1,0:T(8,128)}, bf16[8,288,256]{2,1,0:T(8,128)(2,1)}) custom-call(bf16[8,64,512]{2,1,0:T(8,128)(2,1)} %bitcast.64, bf16[288,256]{1,0:T(8,128)(2,1)} %fusion.17.y_ref), custom_call_target="tpu_custom_call" | custom-call | tf_op jit(solution)/shard_map/pallas_call | solution.py:190
  143.7 1.6 %add_convert_fusion = bf16[64,512]{1,0:T(8,128)(2,1)} fusion(f32[64,512]{1,0:T(8,128)} %get-tuple-element.29, f32[64,1664]{1,0:T(8,128)} %get-tuple-element.27), kind=kLoop, calls=%fused_computation.43 | loop fusion | flops 65536 | bytes 327680 | tf_op jit(solution)/shard_map/convert_element_type | solution.py:480
  145.3 0.9 convert_reduce_fusion
  146.2 1.3 slice.71
  147.5 0.6 slice_bitcast_fusion.1
  148.1 0.2 bitcast_convert_fusion
  148.4 0.6 slice_bitcast_fusion
  149.0 1.4 slice.81
  (21 shorter events, 0.1 us)
Async XLA Ops:
  0.6 65.2 %copy-start = (bf16[256,64]{0,1:T(8,128)(2,1)S(1)}, bf16[256,64]{0,1:T(8,128)(2,1)}, u32[]{:S(2)}) copy-start(bf16[256,64]{0,1:T(8,128)(2,1)} %param.14) | copy-start | bytes 98308
  2.2 41.1 %copy-start.4 = (s32[1024]{0:T(1024)}, s32[1024]{0:T(1024)S(1)}, u32[]{:S(2)}) copy-start(s32[1024]{0:T(1024)S(1)} %fusion.29) | copy-start | bytes 12292
  27.1 16.2 %copy-start.8 = (bf16[16,1024]{1,0:T(8,128)(2,1)S(1)}, bf16[16,1024]{1,0:T(8,128)(2,1)}, u32[]{:S(2)}) copy-start(bf16[16,1024]{1,0:T(8,128)(2,1)} %constant.48.clone.1) | copy-start | bytes 98308
  47.7 18.2 %copy-start.1 = (bf16[4,64,1536]{2,1,0:T(8,128)(2,1)S(1)}, bf16[4,64,1536]{2,1,0:T(8,128)(2,1)}, u32[]{:S(2)}) copy-start(bf16[4,64,1536]{2,1,0:T(8,128)(2,1)} %shard_map.147) | copy-start | bytes 2359300
  47.7 18.2 %copy-start.7 = (bf16[64,512]{1,0:T(8,128)(2,1)S(1)}, bf16[64,512]{1,0:T(8,128)(2,1)}, u32[]{:S(2)}) copy-start(bf16[64,512]{1,0:T(8,128)(2,1)} %param.23) | copy-start | bytes 196612
  90.2 1.5 %copy-start.2 = (bf16[30,64,256]{2,1,0:T(8,128)(2,1)S(1)}, bf16[30,64,256]{2,1,0:T(8,128)(2,1)}, u32[]{:S(2)}) copy-start(bf16[30,64,256]{2,1,0:T(8,128)(2,1)} %get-tuple-element.26) | copy-start | bytes 2949124
  91.6 1.4 copy-start.5
  91.6 1.4 copy-start.6
  93.6 22.6 %copy-start.3 = (s32[1024]{0:T(1024)S(1)}, s32[1024]{0:T(1024)}, u32[]{:S(2)}) copy-start(s32[1024]{0:T(1024)} %add.36) | copy-start | bytes 12292
